TPU v7x, 32 devices: a whole 2x2x4 slice. The times are simulated.
32 devices in a mesh: lat: 8 (over y, x, core), blk: 4 (over z).
Axes of the slice: x: 2, y: 2, z: 4, core: 2. Of those that a mesh axis runs over, the one named last changes fastest.
Arguments:
- mesh_nodes: bfloat16 [10240, 512], P(('lat', 'blk')), may hold values from -6 to 6
- coarse_nodes: bfloat16 [640, 512], replicated, may hold values from -6 to 6
- edge_latents: bfloat16 [65536, 512], P(('lat', 'blk')), may hold values from -6 to 6
- edge_tiles: int32 [512, 2, 128], P(('lat', 'blk')), may hold values from 0 to 1023, as said below
- send_lists: int32 [32, 8, 8], P(('lat', 'blk')), may hold values from 0 to 319
- tiles_live: int32 [32], P(('lat', 'blk')), may hold values from 1 to 16, as said below
- edge_in: bfloat16 [3, 512, 512], replicated, may hold values from -0.15625 to 0.15625
- edge_out: bfloat16 [512, 512], replicated, may hold values from -0.25 to 0.25
- edge_gain: float32 [512], replicated, may hold values from 0.1 to 1.9
- node_in: bfloat16 [2, 512, 512], replicated, may hold values from -0.1875 to 0.1875
- node_out: bfloat16 [512, 512], replicated, may hold values from -0.25 to 0.25
- node_gain: float32 [512], replicated, may hold values from 0.1 to 1.9
- grad_nodes: bfloat16 [10240, 512], P(('lat', 'blk')), may hold values from -6 to 6
- grad_coarse: bfloat16 [640, 512], replicated, may hold values from -6 to 6
- grad_edges: bfloat16 [65536, 512], P(('lat', 'blk')), may hold values from -6 to 6
Outputs:
- new_nodes: bfloat16 [10240, 512], P(('lat', 'blk'))
- new_coarse: bfloat16 [640, 512], replicated
- new_edges: bfloat16 [65536, 512], P(('lat', 'blk'))
- nodes_grad: bfloat16 [10240, 512], P(('lat', 'blk'))
- coarse_grad: bfloat16 [640, 512], replicated
- edges_grad: bfloat16 [65536, 512], P(('lat', 'blk'))
- edge_in_grad: bfloat16 [3, 512, 512], replicated
- edge_out_grad: bfloat16 [512, 512], replicated
- edge_gain_grad: float32 [512], replicated
- node_in_grad: bfloat16 [2, 512, 512], replicated
- node_out_grad: bfloat16 [512, 512], replicated
- node_gain_grad: float32 [512], replicated
Inputs may be any that keep to these rules, and one draw needn't show every extreme that they name: `edge_tiles`: sender entries lie below 1024, receiver entries below 960. `send_lists`: numbers of nodes within the sending block. `tiles_live`: some block has all 16 tiles live.
All inputs are finite; a program needn't handle non-finite values.
Results may differ from a plain program's by a relative error of at most 0.0095.
Values may be sent and summed in bfloat16 or wider, within the bound.
A program may use at most 192 MiB of HBM per device.

v0:
```python
import functools

import jax
import jax.numpy as jnp
from jax import lax
from jax.experimental import pallas as pl
from jax.experimental.pallas import tpu as pltpu
from jax.sharding import PartitionSpec as P

EPS = 1e-05
BF = jnp.bfloat16
F32 = jnp.float32
AXES = ("lat", "blk")
MESH = pl.DeviceIdType.MESH


def dims(a, b, ca, cb):
    return lax.dot_general(a, b, (((ca,), (cb,)), ((), ())), preferred_element_type=F32)


def product(a, b):
    return dims(a, b, 1, 0)


def inner_rows(a, b):
    return dims(a, b, 0, 0)


def outer_cols(a, b):
    return dims(a, b, 1, 1)


def normalize(values):
    centered = values - jnp.mean(values, axis=-1, keepdims=True)
    inverse = lax.rsqrt(jnp.mean(centered * centered, axis=-1, keepdims=True) + EPS)
    return (centered * inverse, inverse)


def normalize_back(upstream, normed, inverse):
    return inverse * (
        upstream
        - jnp.mean(upstream, axis=-1, keepdims=True)
        - normed * jnp.mean(upstream * normed, axis=-1, keepdims=True)
    )


def one_hot(index, shape, axis):
    return jnp.where(lax.broadcasted_iota(jnp.int32, shape, axis) == index, 1.0, 0.0).astype(BF)


def cycle_moves(neigh_count, block_count):
    near_count = neigh_count // 2 - 1
    near = [position - near_count for position in range(near_count)] + [
        position + 1 for position in range(near_count)
    ]
    return near + [block_count // 4, block_count // 2]


def square_bits(sizes):
    found = []
    for axis, size in zip(AXES, sizes):
        step = 1
        while step < size:
            found.append((axis, step))
            step *= 2
        assert step == size
    return found


def turned(bits, turn):
    middle = bits[1:-1]
    turn = turn % len(middle)
    return [bits[0]] + middle[turn:] + middle[:turn] + [bits[-1]]


def bit_of(place, bit):
    return lax.rem(place[bit[0]] // bit[1], 2)


def across(place, bit):
    axis, step = bit
    moved = dict(place)
    moved[axis] = place[axis] + step - 2 * step * bit_of(place, bit)
    return tuple(moved[axis] for axis in AXES)


def here():
    return {axis: lax.axis_index(axis) for axis in AXES}


class Fold:
    def __init__(self, place, order, source, target, lo, rows, cols, arrive, held, sems):
        self.place, self.order = place, order
        self.source, self.target, self.lo = source, target, lo
        self.rows, self.cols = rows, cols
        self.arrive, self.held = arrive, held
        self.rs_send, self.rs_recv, self.ag_send, self.ag_recv = sems

    @staticmethod
    def shapes(count, rows, cols):
        found = []
        for stage in range(count):
            if stage < 2:
                cols //= 2
            else:
                rows //= 2
            found.append((rows, cols))
        return found

    def halves(self, stage):
        rows, cols = self.shapes(len(self.order), self.rows, self.cols)[stage]
        bit = bit_of(self.place, self.order[stage])
        if stage < 2:
            mine, other = pl.multiple_of(bit * cols, 128), pl.multiple_of((1 - bit) * cols, 128)
            return rows, (0, pl.ds(mine, cols)), (0, pl.ds(other, cols))
        mine, other = pl.multiple_of(bit * rows, 16), pl.multiple_of((1 - bit) * rows, 16)
        return rows, (mine, pl.ds(0, cols)), (other, pl.ds(0, cols))

    def previous(self, stage):
        return (self.source, self.lo) if stage == 0 else (self.held[stage - 1], 0)

    def reduce_copy(self, stage):
        rows, _, (start, span) = self.halves(stage)
        ref, base = self.previous(stage)
        return pltpu.make_async_remote_copy(
            src_ref=ref.at[pl.ds(base + start, rows), span],
            dst_ref=self.arrive[stage],
            send_sem=self.rs_send.at[stage],
            recv_sem=self.rs_recv.at[stage],
            device_id=across(self.place, self.order[stage]),
            device_id_type=MESH,
        )

    def add(self, stage):
        rows, (start, span), _ = self.halves(stage)
        ref, base = self.previous(stage)
        last = stage == len(self.order) - 1
        piece = next(size for size in (128, 80, 64, 48, 32, 16) if rows % size == 0)
        if last:
            row_at, col_at = self.corner(len(self.order))
            cols = self.arrive[stage].shape[1]

        def one(step, carry):
            at = pl.multiple_of(step * piece, 16)
            total = ref[pl.ds(base + start + at, piece), span].astype(F32) + self.arrive[stage][
                pl.ds(at, piece), :
            ].astype(F32)
            if last:
                self.target[pl.ds(row_at + at, piece), pl.ds(col_at, cols)] = total.astype(BF)
            else:
                self.held[stage][pl.ds(at, piece), :] = total.astype(BF)
            return carry

        if rows == piece:
            one(0, 0)
        else:
            lax.fori_loop(0, rows // piece, one, 0)

    def corner(self, stages):
        row, col = self.lo, 0
        for stage in range(stages):
            rows, cols = self.shapes(len(self.order), self.rows, self.cols)[stage]
            bit = bit_of(self.place, self.order[stage])
            if stage < 2:
                col = col + bit * cols
            else:
                row = row + bit * rows
        return pl.multiple_of(row, 16), pl.multiple_of(col, 128)

    def gather_copy(self, stage):
        rows, cols = self.shapes(len(self.order), self.rows, self.cols)[stage]
        row, col = self.corner(stage + 1)
        span = self.target.at[pl.ds(row, rows), pl.ds(col, cols)]
        return pltpu.make_async_remote_copy(
            src_ref=span,
            dst_ref=span,
            send_sem=self.ag_send.at[stage],
            recv_sem=self.ag_recv.at[stage],
            device_id=across(self.place, self.order[stage]),
            device_id_type=MESH,
        )


def fold_scratch(count, parts, cols):
    scratch = []
    for _, _, rows, _ in parts:
        shapes = Fold.shapes(count, rows, cols)
        scratch += [pltpu.VMEM(shape, BF) for shape in shapes]
        scratch += [pltpu.VMEM(shape, BF) for shape in shapes[:-1]]
        scratch += [pltpu.SemaphoreType.DMA((count,))] * 4
    return scratch


def make_folds(place, bits, parts, refs, cols):
    count, folds = len(bits), []
    for number, (source, target, rows, lo) in enumerate(parts):
        mine = refs[: 2 * count + 3]
        refs = refs[2 * count + 3 :]
        folds.append(
            Fold(
                place,
                turned(bits, number),
                source,
                target,
                lo,
                rows,
                cols,
                mine[:count],
                mine[count : 2 * count - 1],
                mine[2 * count - 1 :],
            )
        )
    return folds


def fold_all(folds):
    count = len(folds[0].order)
    for stage in range(count):
        copies = [fold.reduce_copy(stage) for fold in folds]
        for copy in copies:
            copy.start()
        for fold, copy in zip(folds, copies):
            copy.wait()
            fold.add(stage)
    for stage in reversed(range(count)):
        copies = [fold.gather_copy(stage) for fold in folds]
        for copy in copies:
            copy.start()
        for copy in copies:
            copy.wait()


def greet(devices):
    barrier = pltpu.get_barrier_semaphore()
    for device in devices:
        pl.semaphore_signal(barrier, inc=1, device_id=device, device_id_type=MESH)
    pl.semaphore_wait(barrier, len(devices))


def split_rows(rows, count, pieces):
    unit = 16 * 2 ** (count - 2)
    units = -(-rows // unit)
    pieces = min(pieces, units)
    sizes = [unit * (units // pieces + (1 if i < units % pieces else 0)) for i in range(pieces)]
    return sizes


def padded(rows, count):
    return sum(split_rows(rows, count, 1))


def block_at(place, sizes, move):
    total = sizes[0] * sizes[1]
    block = lax.rem(place[AXES[0]] * sizes[1] + place[AXES[1]] + (move % total), total)
    return block // sizes[1], lax.rem(block, sizes[1])


def halo_step(sizes, moves, listed_ref, mesh_ref, halo_ref, out, landed, send, recv):
    place = here()
    greet([block_at(place, sizes, move) for move in moves])
    slots = out.shape[1]
    own = mesh_ref.shape[0]
    pick = one_hot(listed_ref[...], (own, listed_ref.shape[1]), 0)
    rows = inner_rows(pick, mesh_ref[...]).astype(BF)
    copies = []
    for k, move in enumerate(moves):
        out[k] = rows[k * slots : (k + 1) * slots]
    for k, move in enumerate(moves):
        copy = pltpu.make_async_remote_copy(
            src_ref=out.at[k],
            dst_ref=landed.at[k],
            send_sem=send.at[k],
            recv_sem=recv.at[k],
            device_id=block_at(place, sizes, -move),
            device_id_type=MESH,
        )
        copy.start()
        copies.append(copy)
    for copy in copies:
        copy.wait()
    halo_ref[...] = landed[...]


def sum_step(bits, lo_rows, part_ref, out_ref, *refs):
    place = here()
    greet([across(place, bit) for bit in bits])
    cols = part_ref.shape[1]
    parts, lo = [], 0
    for rows in lo_rows:
        parts.append((part_ref, out_ref, rows, lo))
        lo += rows
    fold_all(make_folds(place, bits, parts, refs, cols))


def final_step(
    bits,
    sizes,
    moves,
    lo_rows,
    edge_ref,
    node_ref,
    term_ref,
    listed_ref,
    direct_ref,
    edge_out,
    node_out,
    nodes_grad,
    landed,
    send,
    recv,
    *refs,
):
    place = here()
    greet([across(place, bit) for bit in bits] + [block_at(place, sizes, -move) for move in moves])
    copies = []
    for k, move in enumerate(moves):
        copy = pltpu.make_async_remote_copy(
            src_ref=term_ref.at[k],
            dst_ref=landed.at[k],
            send_sem=send.at[k],
            recv_sem=recv.at[k],
            device_id=block_at(place, sizes, move),
            device_id_type=MESH,
        )
        copy.start()
        copies.append(copy)
    cols = edge_ref.shape[1]
    parts, lo = [], 0
    for rows in lo_rows:
        parts.append((edge_ref, edge_out, rows, lo))
        lo += rows
    parts.append((node_ref, node_out, node_ref.shape[0], 0))
    folds = make_folds(place, bits, parts, refs, cols)
    fold_all(folds)
    for copy in copies:
        copy.wait()
    own = direct_ref.shape[0]
    pick = one_hot(listed_ref[...], (own, listed_ref.shape[1]), 0)
    back = landed[...].reshape(listed_ref.shape[1], cols)
    nodes_grad[...] = (direct_ref[...] + product(pick, back)).astype(BF)


def edge_index(tiles_ref, own, halo):
    count, _, width = tiles_ref.shape
    flat = tiles_ref[...].reshape(2 * count, width)
    fine = jnp.where(flat < own, flat, flat + halo)
    row = lax.broadcasted_iota(jnp.int32, flat.shape, 0)
    flat = jnp.where(lax.rem(row, 2) == 0, flat, fine)
    turned_flat = flat.T
    send_col = jnp.concatenate([turned_flat[:, 2 * t : 2 * t + 1] for t in range(count)], axis=0)
    recv_col = jnp.concatenate([turned_flat[:, 2 * t + 1 : 2 * t + 2] for t in range(count)], axis=0)
    send_row = jnp.concatenate([flat[2 * t : 2 * t + 1, :] for t in range(count)], axis=1)
    recv_row = jnp.concatenate([flat[2 * t + 1 : 2 * t + 2, :] for t in range(count)], axis=1)
    return send_col, recv_col, send_row, recv_row


def edge_forward(
    tile_width,
    live_ref,
    lat_ref,
    tiles_ref,
    mesh_ref,
    halo_ref,
    coarse_ref,
    win_ref,
    wout_ref,
    gain_ref,
    new_ref,
    hid_ref,
    slope_ref,
    norm_ref,
    inv_ref,
    agg_own,
    agg_coarse,
    proj_s,
    proj_r,
    agg,
):
    step = pl.program_id(0)
    own, halo = mesh_ref.shape[0], halo_ref.shape[0]
    rows = agg.shape[0]
    block = lat_ref.shape[0]

    @pl.when(step == 0)
    def _():
        agg[...] = jnp.zeros_like(agg)
        for part, lo in ((mesh_ref, 0), (halo_ref, own), (coarse_ref, own + halo)):
            span = pl.ds(lo, part.shape[0])
            proj_s[span, :] = product(part[...], win_ref[1]).astype(BF)
            proj_r[span, :] = product(part[...], win_ref[2]).astype(BF)

    send_col, recv_col, _, recv_row = edge_index(tiles_ref, own, halo)
    rows_in = lat_ref[...]
    pre = (
        product(rows_in, win_ref[0])
        + product(one_hot(send_col, (block, rows), 1), proj_s[...])
        + product(one_hot(recv_col, (block, rows), 1), proj_r[...])
    )
    sig = 1.0 / (1.0 + jnp.exp(-pre))
    hidden = (pre * sig).astype(BF)
    slope_ref[...] = (sig * (1.0 + pre * (1.0 - sig))).astype(BF)
    hid_ref[...] = hidden
    normed, inverse = normalize(product(hidden, wout_ref[...]))
    norm_ref[...] = normed.astype(BF)
    inv_ref[...] = inverse
    place = step * block + lax.broadcasted_iota(jnp.int32, (block, 1), 0)
    alive = jnp.where(place < live_ref[0] * tile_width, 1.0, 0.0)
    message = normed * gain_ref[...] * alive
    new_ref[...] = (rows_in.astype(F32) + message).astype(BF)
    agg[...] += product(one_hot(recv_row, (rows, block), 0), message.astype(BF))

    @pl.when(step == pl.num_programs(0) - 1)
    def _():
        agg_own[...] = agg[pl.ds(0, own), :].astype(BF)
        agg_coarse[...] = agg[pl.ds(own + halo, rows - own - halo), :].astype(BF)


def edge_backward(
    tile_width,
    factor,
    live_ref,
    lat_ref,
    grad_ref,
    hid_ref,
    slope_ref,
    norm_ref,
    inv_ref,
    tiles_ref,
    mesh_ref,
    halo_ref,
    coarse_ref,
    own_slope,
    coarse_slope,
    own_direct,
    coarse_direct,
    win_ref,
    wout_ref,
    gain_ref,
    edges_grad,
    pack,
    own_term,
    halo_term,
    table,
    sent,
    received,
    first_acc,
    out_acc,
    gain_grad,
):
    step = pl.program_id(0)
    own, halo = mesh_ref.shape[0], halo_ref.shape[0]
    rows = table.shape[0]
    block = lat_ref.shape[0]

    @pl.when(step == 0)
    def _():
        for acc in (sent, received, first_acc, out_acc, gain_grad):
            acc[...] = jnp.zeros_like(acc)
        table[pl.ds(0, own), :] = own_slope[...]
        table[pl.ds(own, halo), :] = jnp.zeros((halo, table.shape[1]), BF)
        table[pl.ds(own + halo, rows - own - halo), :] = coarse_slope[...]

    _, recv_col, send_row, recv_row = edge_index(tiles_ref, own, halo)
    place = step * block + lax.broadcasted_iota(jnp.int32, (block, 1), 0)
    alive = jnp.where(place < live_ref[0] * tile_width, 1.0, 0.0)
    edge_slope = grad_ref[...].astype(F32)
    message_slope = (
        edge_slope + product(one_hot(recv_col, (block, rows), 1), table[...])
    ) * alive
    normed = norm_ref[...].astype(F32)
    gain_grad[...] += jnp.sum(message_slope * normed, axis=0, keepdims=True)
    out_slope = normalize_back(message_slope * gain_ref[...], normed, inv_ref[...]).astype(BF)
    out_acc[...] += inner_rows(hid_ref[...], out_slope)
    pre_slope = (outer_cols(out_slope, wout_ref[...]) * slope_ref[...].astype(F32)).astype(BF)
    edges_grad[...] = (edge_slope + outer_cols(pre_slope, win_ref[0])).astype(BF)
    first_acc[...] += inner_rows(lat_ref[...], pre_slope)
    sent[...] += product(one_hot(send_row, (rows, block), 0), pre_slope)
    received[...] += product(one_hot(recv_row, (rows, block), 0), pre_slope)

    @pl.when(step == pl.num_programs(0) - 1)
    def _():
        d = first_acc.shape[0]
        coarse = coarse_ref.shape[0]
        pack[pl.ds(0, d), :] = (first_acc[...] * factor).astype(BF)
        pack[pl.ds(3 * d, d), :] = (out_acc[...] * factor).astype(BF)
        sums = [None, None]
        for part, lo in ((mesh_ref, 0), (halo_ref, own), (coarse_ref, own + halo)):
            span = pl.ds(lo, part.shape[0])
            total = None
            for which, source in enumerate((sent, received)):
                piece = source[span, :].astype(BF)
                weight = inner_rows(part[...], piece)
                sums[which] = weight if sums[which] is None else sums[which] + weight
                back = outer_cols(piece, win_ref[1 + which])
                total = back if total is None else total + back
            if part is mesh_ref:
                own_term[...] = total + own_direct[...]
            elif part is halo_ref:
                halo_term[...] = total.astype(BF)
            else:
                pack[pl.ds(4 * d, coarse), :] = (total + coarse_direct[...]).astype(BF)
        pack[pl.ds(d, d), :] = (sums[0] * factor).astype(BF)
        pack[pl.ds(2 * d, d), :] = (sums[1] * factor).astype(BF)
        rest = pack.shape[0] - 4 * d - coarse
        pack[pl.ds(4 * d + coarse, rest), :] = jnp.broadcast_to(gain_grad[...] * factor, (rest, d)).astype(BF)


def node_step(
    masked,
    factor,
    me_ref,
    rows_ref,
    sum_ref,
    grad_ref,
    win_ref,
    wout_ref,
    gain_ref,
    *refs,
):
    if masked:
        base, new_ref, direct_ref, agg_grad, pack, in_grad, out_grad, gain_grad = refs
    else:
        new_ref, direct_ref, agg_grad, in_grad, out_grad, gain_grad = refs

    @pl.when(pl.program_id(0) == 0)
    def _():
        for acc in (in_grad, out_grad, gain_grad):
            acc[...] = jnp.zeros_like(acc)

    rows = rows_ref[...]
    summed = sum_ref[...]
    pre = product(rows, win_ref[0]) + product(summed, win_ref[1])
    sig = 1.0 / (1.0 + jnp.exp(-pre))
    hidden = (pre * sig).astype(BF)
    normed, inverse = normalize(product(hidden, wout_ref[...]))
    new_ref[...] = (rows.astype(F32) + normed * gain_ref[...]).astype(BF)
    node_slope = grad_ref[...].astype(F32)
    out_slope = normalize_back(node_slope * gain_ref[...], normed, inverse).astype(BF)
    swish = sig * (1.0 + pre * (1.0 - sig))
    pre_slope = (outer_cols(out_slope, wout_ref[...]) * swish).astype(BF)
    agg_grad[...] = outer_cols(pre_slope, win_ref[1]).astype(BF)
    direct = node_slope + outer_cols(pre_slope, win_ref[0])
    if masked:
        count, block = me_ref[1], rows.shape[0]
        place = pl.program_id(0) * block + lax.broadcasted_iota(jnp.int32, (block, 1), 0)
        share = jnp.where((place * count) // (pl.num_programs(0) * block) == me_ref[0], 1.0, 0.0)
        direct = direct * share
        node_slope = node_slope * share
        hidden = (hidden.astype(F32) * share).astype(BF)
        pre_slope = (pre_slope.astype(F32) * share).astype(BF)
    direct_ref[...] = direct
    gain_grad[...] += jnp.sum(node_slope * normed, axis=0, keepdims=True)
    out_grad[...] += inner_rows(hidden, out_slope)
    in_grad[0] += inner_rows(rows, pre_slope)
    in_grad[1] += inner_rows(summed, pre_slope)
    if masked:

        @pl.when(pl.program_id(0) == pl.num_programs(0) - 1)
        def _():
            d = in_grad.shape[1]
            for i in range(2):
                pack[pl.ds(i * d, d), :] = ((in_grad[i] + base[pl.ds(i * d, d), :]) * factor).astype(BF)
            pack[pl.ds(2 * d, d), :] = ((out_grad[...] + base[pl.ds(2 * d, d), :]) * factor).astype(BF)
            rest = pack.shape[0] - 3 * d
            gain = (gain_grad[...] + base[pl.ds(3 * d, 1), :]) * factor
            pack[pl.ds(3 * d, rest), :] = jnp.broadcast_to(gain, (rest, d)).astype(BF)


def whole(shape):
    zero = (0,) * len(shape)
    return pl.BlockSpec(shape, lambda i: zero)


def by_rows(block, width):
    return pl.BlockSpec((block, width), lambda i: (i, 0))


def by_cols(block):
    return pl.BlockSpec((1, block), lambda i: (0, i))


def shape_of(shape, dtype):
    return jax.ShapeDtypeStruct(shape, dtype)


def cost(flops, moved):
    return pl.CostEstimate(flops=int(flops), bytes_accessed=int(moved), transcendentals=0)


PARAMS = dict(
    compiler_params=pltpu.CompilerParams(
        dimension_semantics=("arbitrary",), vmem_limit_bytes=60 * 1024 * 1024
    )
)


def talking(number):
    return pltpu.CompilerParams(
        collective_id=number, has_side_effects=True, vmem_limit_bytes=60 * 1024 * 1024
    )


def node_call(me, rows, summed, grad, node_in, node_out, gain, block, factor, base=None, pack_rows=0):
    count, d = rows.shape
    row = by_rows(block, d)
    masked = base is not None
    smem = pl.BlockSpec(memory_space=pltpu.SMEM)
    accs = [(2, d, d), (d, d), (1, d)]
    extra_in = [whole(base.shape)] if masked else []
    acc_specs = [whole((pack_rows, d))] if masked else [whole(shape) for shape in accs]
    acc_shapes = [shape_of((pack_rows, d), BF)] if masked else [shape_of(shape, F32) for shape in accs]
    return pl.pallas_call(
        functools.partial(node_step, masked, factor),
        grid=(count // block,),
        in_specs=[smem, row, row, row, whole((2, d, d)), whole((d, d)), whole((1, d))] + extra_in,
        out_specs=[row, row, row] + acc_specs,
        out_shape=[shape_of((count, d), BF), shape_of((count, d), F32), shape_of((count, d), BF)] + acc_shapes,
        scratch_shapes=[pltpu.VMEM(shape, F32) for shape in accs] if masked else [],
        cost_estimate=cost(18 * count * d * d, 12 * count * d),
        **PARAMS,
    )(me, rows, summed, grad, node_in, node_out, gain, *([base] if masked else []))


def on_device(
    mesh_nodes,
    coarse_nodes,
    edge_latents,
    edge_tiles,
    send_lists,
    tiles_live,
    edge_in,
    edge_out,
    edge_gain,
    node_in,
    node_out,
    node_gain,
    grad_nodes,
    grad_coarse,
    grad_edges,
):
    sizes = tuple(lax.axis_size(axis) for axis in AXES)
    block_count = sizes[0] * sizes[1]
    bits = square_bits(sizes)
    count = len(bits)
    own, d = mesh_nodes.shape
    neigh, slots = send_lists.shape[1:]
    coarse = coarse_nodes.shape[0]
    halo = neigh * slots
    rows = own + halo + coarse
    tile_dev, _, tile_width = edge_tiles.shape
    edges = tile_dev * tile_width
    tiles = 4 if tile_dev % 4 == 0 else 1
    block = tiles * tile_width
    moves = cycle_moves(neigh, block_count)
    factor = float(edges * block_count) ** (-0.5)
    listed = send_lists.reshape(1, halo)
    me = jnp.stack([lax.axis_index("lat") * sizes[1] + lax.axis_index("blk"), jnp.int32(block_count)])
    e_gain, n_gain = edge_gain.reshape(1, d), node_gain.reshape(1, d)
    vmem = pl.BlockSpec(memory_space=pltpu.VMEM)
    incoming = pl.pallas_call(
        functools.partial(halo_step, sizes, moves),
        in_specs=[vmem, vmem],
        out_specs=vmem,
        out_shape=shape_of((neigh, slots, d), BF),
        scratch_shapes=[pltpu.VMEM((neigh, slots, d), BF)] * 2 + [pltpu.SemaphoreType.DMA((neigh,))] * 2,
        compiler_params=talking(0),
    )(listed, mesh_nodes).reshape(halo, d)

    smem = pl.BlockSpec(memory_space=pltpu.SMEM)
    wide, col = by_rows(block, d), by_rows(block, 1)
    pairs = pl.BlockSpec((tiles, 2, tile_width), lambda i: (i, 0, 0))
    tables = [whole((own, d)), whole((halo, d)), whole((coarse, d))]
    weights = [whole((3, d, d)), whole((d, d)), whole((1, d))]
    new_edges, hidden, slope, normed, inverse, agg_own, agg_coarse = pl.pallas_call(
        functools.partial(edge_forward, tile_width),
        grid=(edges // block,),
        in_specs=[smem, wide, pairs] + tables + weights,
        out_specs=[wide] * 4 + [col, whole((own, d)), whole((coarse, d))],
        out_shape=[shape_of((edges, d), BF)] * 4
        + [shape_of((edges, 1), F32), shape_of((own, d), BF), shape_of((coarse, d), BF)],
        scratch_shapes=[
            pltpu.VMEM((rows, d), BF),
            pltpu.VMEM((rows, d), BF),
            pltpu.VMEM((rows, d), F32),
        ],
        cost_estimate=cost(2 * edges * d * (3 * rows + 2 * d), 12 * edges * d),
        **PARAMS,
    )(tiles_live, edge_latents, edge_tiles, mesh_nodes, incoming, coarse_nodes, edge_in, edge_out, e_gain)
    sum_rows = padded(coarse, count)
    if sum_rows > coarse:
        agg_coarse = jnp.pad(agg_coarse, ((0, sum_rows - coarse), (0, 0)))
    coarse_rows = split_rows(sum_rows, count, 3)
    coarse_parts = [(None, None, part, 0) for part in coarse_rows]
    coarse_total = pl.pallas_call(
        functools.partial(sum_step, bits, coarse_rows),
        in_specs=[vmem],
        out_specs=vmem,
        out_shape=shape_of((sum_rows, d), BF),
        scratch_shapes=fold_scratch(count, coarse_parts, d),
        compiler_params=talking(1),
    )(agg_coarse)[:coarse]
    new_nodes, own_direct, own_slope, own_in, own_out, own_ngain = node_call(
        me, mesh_nodes, agg_own, grad_nodes, node_in, node_out, n_gain, own, factor
    )
    base = jnp.concatenate([own_in.reshape(2 * d, d), own_out, jnp.broadcast_to(own_ngain, (8, d))], axis=0)
    c_block = own if coarse % own == 0 else coarse
    node_rows = padded(3 * d + 1, count)
    new_coarse, c_direct, c_slope, node_pack = node_call(
        me, coarse_nodes, coarse_total, grad_coarse, node_in, node_out, n_gain, c_block, factor, base, node_rows
    )
    edge_rows = padded(4 * d + coarse + 1, count)
    edges_grad, edge_pack, own_term, halo_term = pl.pallas_call(
        functools.partial(edge_backward, tile_width, factor),
        grid=(edges // block,),
        in_specs=[smem] + [wide] * 5 + [col, pairs] + tables
        + [whole((own, d)), whole((coarse, d))] * 2 + weights,
        out_specs=[wide, whole((edge_rows, d)), whole((own, d)), whole((halo, d))],
        out_shape=[
            shape_of((edges, d), BF),
            shape_of((edge_rows, d), BF),
            shape_of((own, d), F32),
            shape_of((halo, d), BF),
        ],
        scratch_shapes=[
            pltpu.VMEM((rows, d), BF),
            pltpu.VMEM((rows, d), F32),
            pltpu.VMEM((rows, d), F32),
            pltpu.VMEM((d, d), F32),
            pltpu.VMEM((d, d), F32),
            pltpu.VMEM((1, d), F32),
        ],
        cost_estimate=cost(2 * edges * d * (3 * rows + 4 * d), 14 * edges * d),
        **PARAMS,
    )(
        tiles_live, edge_latents, grad_edges, hidden, slope, normed, inverse, edge_tiles, mesh_nodes, incoming,
        coarse_nodes, own_slope, c_slope, own_direct, c_direct, edge_in, edge_out, e_gain,
    )
    cuts = split_rows(edge_rows, count, 2)
    parts = [(None, None, part, 0) for part in cuts + [node_rows]]
    edge_sum, node_sum, nodes_grad = pl.pallas_call(
        functools.partial(final_step, bits, sizes, moves, cuts),
        in_specs=[vmem] * 5,
        out_specs=[vmem] * 3,
        out_shape=[shape_of((edge_rows, d), BF), shape_of((node_rows, d), BF), shape_of((own, d), BF)],
        scratch_shapes=[pltpu.VMEM((neigh, slots, d), BF)]
        + [pltpu.SemaphoreType.DMA((neigh,))] * 2
        + fold_scratch(count, parts, d),
        compiler_params=talking(2),
    )(edge_pack, node_pack, halo_term.reshape(neigh, slots, d), listed, own_term)
    return (
        new_nodes,
        new_coarse,
        new_edges,
        nodes_grad,
        edge_sum[4 * d : 4 * d + coarse],
        edges_grad,
        edge_sum[: 3 * d].reshape(3, d, d),
        edge_sum[3 * d : 4 * d],
        edge_sum[4 * d + coarse].astype(F32),
        node_sum[: 2 * d].reshape(2, d, d),
        node_sum[2 * d : 3 * d],
        node_sum[3 * d].astype(F32),
    )


def solution(mesh):
    rows2 = P(AXES, None)
    rows3 = P(AXES, None, None)
    in_specs = (
        rows2, P(), rows2, rows3, rows3, P(AXES), P(), P(), P(), P(), P(), P(), rows2, P(), rows2,
    )
    out_specs = (rows2, P(), rows2, rows2, P(), rows2, P(), P(), P(), P(), P(), P())
    return jax.shard_map(
        on_device, mesh=mesh, in_specs=in_specs, out_specs=out_specs, check_vma=False
    )
```

profile of v0, /device:TPU:0, one launch (start us, length us, event | category | flops | bytes accessed | tf_op | source)
XLA Modules:
  0.0 189.7 jit_solution(5781260670493449722)
XLA Ops:
  1.3 0.6 pad_add_fusion.me_ref
  1.9 1.3 reshape.52.listed_ref
  3.2 11.6 %shard_map.238 = bf16[8,8,512]{2,1,0:T(8,128)(2,1)} custom-call(s32[1,64]{1,0:T(1,128)} %reshape.52.listed_ref, bf16[320,512]{1,0:T(8,128)(2,1)} %mesh_ref.5), custom_call_target="tpu_custom_call" | custom-call | tf_op jit(solution)/shard_map/pallas_call | solution.py:660
  14.8 18.4 %shard_map.239 = (bf16[2048,512]{1,0:T(8,128)(2,1)}, bf16[2048,512]{1,0:T(8,128)(2,1)}, bf16[2048,512]{1,0:T(8,128)(2,1)}, bf16[2048,512]{1,0:T(8,128)(2,1)}, f3...) custom-call(s32[1]{0:T(128)S(6)} %copy.28.live_ref, bf16[2048,512]{1,0:T(8,128)(2,1)} %lat_ref.3, ...), custom_call_target="tpu_custom_call" | custom-call | flops 8589934592 | bytes 12582912 | tf_op jit(solution)/shard_map/pallas_call | solution.py:674
  33.1 31.7 %shard_map.241.sum_ref = bf16[640,512]{1,0:T(8,128)(2,1)} custom-call(bf16[640,512]{1,0:T(8,128)(2,1)} %get-tuple-element.38.part_ref), custom_call_target="tpu_custom_call" | custom-call | tf_op jit(solution)/shard_map/pallas_call | solution.py:694
  64.9 6.1 %shard_map.240 = (bf16[320,512]{1,0:T(8,128)(2,1)}, f32[320,512]{1,0:T(8,128)}, bf16[320,512]{1,0:T(8,128)(2,1)}, f32[2,512,512]{2,1,0:T(8,128)}, f32[512,512]{1,0:T(8,128)}, /*index=5*/f32[1,512]{1,0:T(1,128)}) custom-call(s32[2]{0:T(128)} %pad_add_fusion.me_ref, bf16[320,512]{1,0:T(8,128)(2,1)} %mesh_ref.5, bf16[320,512]{1,0:T(8,128)(2,1)} %get-tuple-element.36.sum_ref, ...), custom_call_target="tpu_custom_call" | custom-call | flops 1509949440 | bytes 1966080 | tf_op jit(solution)/shard_map/pallas_call | solution.py:612
  71.0 0.7 broadcast_in_dim.8
  71.6 3.9 %pad_maximum_fusion.refs_0_ = f32[1544,512]{1,0:T(8,128)} fusion(f32[8,512]{1,0:T(8,128)S(1)} %broadcast_in_dim.8, f32[512,512]{1,0:T(8,128)} %get-tuple-element.40, f32[1024,512]{1,0:T(8,128)} %bitcast.11), kind=kLoop, calls=%fused_computation | loop fusion | flops 1581056 | bytes 6324224 | tf_op jit(solution)/shard_map/concatenate | solution.py:705
  75.5 10.6 %shard_map.242 = (bf16[640,512]{1,0:T(8,128)(2,1)}, f32[640,512]{1,0:T(8,128)}, bf16[640,512]{1,0:T(8,128)(2,1)}, bf16[1664,512]{1,0:T(8,128)(2,1)}) custom-call(s32[2]{0:T(128)} %pad_add_fusion.me_ref, bf16[640,512]{1,0:T(8,128)(2,1)} %coarse_ref.3, bf16[640,512]{1,0:T(8,128)(2,1)} %shard_map.241.sum_ref, bf16[640,512]{1,0:T(8,128)(2,1)} %grad_ref.4, ...), custom_call_target="tpu_custom_call" | custom-call | flops 3019898880 | bytes 3932160 | tf_op jit(solution)/shard_map/pallas_call | solution.py:612
  86.1 24.6 %shard_map.243 = (bf16[2048,512]{1,0:T(8,128)(2,1)}, bf16[2816,512]{1,0:T(8,128)(2,1)}, f32[320,512]{1,0:T(8,128)}, bf16[64,512]{1,0:T(8,128)(2,1)}) custom-call(s32[1]{0:T(128)S(6)} %copy.28.live_ref, bf16[2048,512]{1,0:T(8,128)(2,1)} %lat_ref.3, bf16[2048,512]{1,0:T(8,128)(2,1)} %grad_ref.5, bf16[2048,512]{1,0:T(8,128)(2,1)} %get-tuple-element.44.hid_ref, ...), custom_call_target="tpu_custom_call" | custom-call | flops 10737418240 | bytes 14680064 | tf_op jit(solution)/shard_map/pallas_call | solution.py:712
  110.7 69.8 %shard_map.244 = (bf16[2816,512]{1,0:T(8,128)(2,1)}, bf16[1664,512]{1,0:T(8,128)(2,1)}, bf16[320,512]{1,0:T(8,128)(2,1)}) custom-call(bf16[2816,512]{1,0:T(8,128)(2,1)} %get-tuple-element.52.edge_ref, bf16[1664,512]{1,0:T(8,128)(2,1)} %get-tuple-element.53.node_ref, bf16[8,8,512]{2,1,0:T(8,128)(2,1)} %bitcast.14, s32[1,64]{1,0:T(1,128)} %reshape.52.listed_ref, ...), custom_call_target="tpu_custom_call" | custom-call | tf_op jit(solution)/shard_map/pallas_call | solution.py:740
  180.4 0.0 copy-start
  180.4 1.4 slice_convert_fusion
  181.9 1.9 slice.26
  183.8 2.3 %slice.25 = bf16[1024,512]{1,0:T(8,128)(2,1)} slice(bf16[1664,512]{1,0:T(8,128)(2,1)} %get-tuple-element.59), slice={[0:1024], [0:512]} | slice | bytes 2097152 | tf_op jit(solution)/shard_map/slice | solution.py:760
  186.0 0.0 copy-done
  186.0 0.8 slice.23
  186.8 0.0 copy-start.1
  186.8 0.9 slice.21
  187.7 1.2 slice.22
  189.0 0.0 copy-done.1
  189.0 0.7 copy.29
Async XLA Ops:
  180.4 5.6 %copy-start = (bf16[2816,512]{1,0:T(8,128)(2,1)S(1)}, bf16[2816,512]{1,0:T(8,128)(2,1)}, u32[]{:S(2)}) copy-start(bf16[2816,512]{1,0:T(8,128)(2,1)} %get-tuple-element.57) | copy-start | bytes 8650756
  186.8 2.1 %copy-start.1 = (bf16[320,512]{1,0:T(8,128)(2,1)S(1)}, bf16[320,512]{1,0:T(8,128)(2,1)}, u32[]{:S(2)}) copy-start(bf16[320,512]{1,0:T(8,128)(2,1)} %get-tuple-element.77) | copy-start | bytes 983044
where the time goes:
time: 190 us
  Pallas kernels  173 us (91%)
  local copies, waits for them, and re-layouts  9.77 us (5%)
  other arithmetic  5.91 us (3%)
    pallas_call x1, Pallas kernels, on_device(): pl.pallas_call(functools.partial(final_step, bits, sizes, moves, cuts), i...  69.8 us
    pallas_call x1, Pallas kernels, on_device(): pl.pallas_call(functools.partial(sum_step, bits, coarse_rows), in_specs=[...  31.7 us
    pallas_call x1, Pallas kernels, on_device(): pl.pallas_call(functools.partial(edge_backward, tile_width, factor), grid...  24.6 us
    pallas_call x1, Pallas kernels, on_device(): pl.pallas_call(functools.partial(edge_forward, tile_width), grid=(edges /...  18.4 us
    pallas_call x2, Pallas kernels, node_call(): pl.pallas_call(functools.partial(node_step, masked, factor), grid=(count...  16.7 us
    pallas_call x1, Pallas kernels, on_device(): pl.pallas_call(functools.partial(halo_step, sizes, moves), in_specs=[vmem...  11.6 us
    concatenate x1, other arithmetic, on_device(): jnp.concatenate([own_in.reshape(2 * d, d), own_out, jnp.broadcast_to(own_...  3.87 us

commit v1 on v0

--- a/solution.py
+++ b/solution.py
@@ -89,28 +89,42 @@
 
 
 class Fold:
-    def __init__(self, place, order, source, target, lo, rows, cols, arrive, held, sems):
-        self.place, self.order = place, order
+    def __init__(self, place, order, kinds, source, target, lo, rows, cols, refs, wide_first=False):
+        count = len(order)
+        self.place, self.order, self.kinds = place, order, kinds
         self.source, self.target, self.lo = source, target, lo
         self.rows, self.cols = rows, cols
-        self.arrive, self.held = arrive, held
-        self.rs_send, self.rs_recv, self.ag_send, self.ag_recv = sems
+        self.arrive, self.held = refs[:count], refs[count : 2 * count - 1]
+        self.rs_send, self.rs_recv, self.ag_send, self.ag_recv = refs[2 * count - 1 : 2 * count + 3]
+        self.sizes = Fold.shapes(kinds, rows, cols)
+        self.gather_order = list(reversed(range(count)))
+        if wide_first:
+            self.gather_order.sort(key=lambda stage: kinds[stage] == "r")
 
     @staticmethod
-    def shapes(count, rows, cols):
+    def shapes(kinds, rows, cols):
         found = []
-        for stage in range(count):
-            if stage < 2:
+        for kind in kinds:
+            if kind == "c":
                 cols //= 2
             else:
                 rows //= 2
             found.append((rows, cols))
         return found
 
+    @staticmethod
+    def scratch(kinds, rows, cols):
+        shapes, count = Fold.shapes(kinds, rows, cols), len(kinds)
+        return (
+            [pltpu.VMEM(shape, BF) for shape in shapes]
+            + [pltpu.VMEM(shape, BF) for shape in shapes[:-1]]
+            + [pltpu.SemaphoreType.DMA((count,))] * 4
+        )
+
     def halves(self, stage):
-        rows, cols = self.shapes(len(self.order), self.rows, self.cols)[stage]
+        rows, cols = self.sizes[stage]
         bit = bit_of(self.place, self.order[stage])
-        if stage < 2:
+        if self.kinds[stage] == "c":
             mine, other = pl.multiple_of(bit * cols, 128), pl.multiple_of((1 - bit) * cols, 128)
             return rows, (0, pl.ds(mine, cols)), (0, pl.ds(other, cols))
         mine, other = pl.multiple_of(bit * rows, 16), pl.multiple_of((1 - bit) * rows, 16)
@@ -131,14 +145,28 @@
             device_id_type=MESH,
         )
 
+    def region(self, pending):
+        row, col, rows, cols = self.lo, 0, self.rows, self.cols
+        for stage in pending:
+            bit = bit_of(self.place, self.order[stage])
+            if self.kinds[stage] == "c":
+                cols //= 2
+                col = col + bit * cols
+            else:
+                rows //= 2
+                row = row + bit * rows
+        return pl.ds(pl.multiple_of(row, 16), rows), pl.ds(pl.multiple_of(col, 128), cols)
+
+    def pending(self, stage):
+        return sorted(self.gather_order[self.gather_order.index(stage) :])
+
     def add(self, stage):
         rows, (start, span), _ = self.halves(stage)
         ref, base = self.previous(stage)
         last = stage == len(self.order) - 1
-        piece = next(size for size in (128, 80, 64, 48, 32, 16) if rows % size == 0)
+        piece = next(size for size in (128, 96, 80, 64, 48, 32, 16) if rows % size == 0)
         if last:
-            row_at, col_at = self.corner(len(self.order))
-            cols = self.arrive[stage].shape[1]
+            row_at, col_at = self.region(range(len(self.order)))
 
         def one(step, carry):
             at = pl.multiple_of(step * piece, 16)
@@ -146,7 +174,7 @@
                 pl.ds(at, piece), :
             ].astype(F32)
             if last:
-                self.target[pl.ds(row_at + at, piece), pl.ds(col_at, cols)] = total.astype(BF)
+                self.target[pl.ds(pl.multiple_of(row_at.start + at, 16), piece), col_at] = total.astype(BF)
             else:
                 self.held[stage][pl.ds(at, piece), :] = total.astype(BF)
             return carry
@@ -156,78 +184,67 @@
         else:
             lax.fori_loop(0, rows // piece, one, 0)
 
-    def corner(self, stages):
-        row, col = self.lo, 0
-        for stage in range(stages):
-            rows, cols = self.shapes(len(self.order), self.rows, self.cols)[stage]
-            bit = bit_of(self.place, self.order[stage])
-            if stage < 2:
-                col = col + bit * cols
-            else:
-                row = row + bit * rows
-        return pl.multiple_of(row, 16), pl.multiple_of(col, 128)
-
-    def gather_copy(self, stage):
-        rows, cols = self.shapes(len(self.order), self.rows, self.cols)[stage]
-        row, col = self.corner(stage + 1)
-        span = self.target.at[pl.ds(row, rows), pl.ds(col, cols)]
+    def gather_copy(self, stage, target=None, sems=None):
+        span = (self.target if target is None else target).at[self.region(self.pending(stage))]
+        send, recv = (self.ag_send, self.ag_recv) if sems is None else sems
         return pltpu.make_async_remote_copy(
             src_ref=span,
             dst_ref=span,
-            send_sem=self.ag_send.at[stage],
-            recv_sem=self.ag_recv.at[stage],
+            send_sem=send.at[stage],
+            recv_sem=recv.at[stage],
             device_id=across(self.place, self.order[stage]),
             device_id_type=MESH,
         )
 
 
-def fold_scratch(count, parts, cols):
+def sum_kinds(count):
+    return ["c", "c"] + ["r"] * (count - 2)
+
+
+def coarse_kinds(count):
+    return ["r", "c", "c"] + ["r"] * (count - 3)
+
+
+def fold_scratch(kinds, rows, cols):
     scratch = []
-    for _, _, rows, _ in parts:
-        shapes = Fold.shapes(count, rows, cols)
-        scratch += [pltpu.VMEM(shape, BF) for shape in shapes]
-        scratch += [pltpu.VMEM(shape, BF) for shape in shapes[:-1]]
-        scratch += [pltpu.SemaphoreType.DMA((count,))] * 4
+    for part in rows:
+        scratch += Fold.scratch(kinds, part, cols)
     return scratch
 
 
-def make_folds(place, bits, parts, refs, cols):
+def make_folds(place, bits, kinds, parts, refs, cols, wide_first=False):
     count, folds = len(bits), []
     for number, (source, target, rows, lo) in enumerate(parts):
-        mine = refs[: 2 * count + 3]
-        refs = refs[2 * count + 3 :]
-        folds.append(
-            Fold(
-                place,
-                turned(bits, number),
-                source,
-                target,
-                lo,
-                rows,
-                cols,
-                mine[:count],
-                mine[count : 2 * count - 1],
-                mine[2 * count - 1 :],
-            )
-        )
+        mine, refs = refs[: 2 * count + 3], refs[2 * count + 3 :]
+        folds.append(Fold(place, turned(bits, number), kinds, source, target, lo, rows, cols, mine, wide_first))
     return folds
+
+
+def cut_parts(source, target, sizes):
+    parts, lo = [], 0
+    for rows in sizes:
+        parts.append((source, target, rows, lo))
+        lo += rows
+    return parts
 
 
 def fold_all(folds):
     count = len(folds[0].order)
+    for fold in folds:
+        fold.reduce_copy(0).start()
     for stage in range(count):
-        copies = [fold.reduce_copy(stage) for fold in folds]
-        for copy in copies:
-            copy.start()
-        for fold, copy in zip(folds, copies):
-            copy.wait()
+        for fold in folds:
+            fold.reduce_copy(stage).wait()
             fold.add(stage)
-    for stage in reversed(range(count)):
-        copies = [fold.gather_copy(stage) for fold in folds]
-        for copy in copies:
-            copy.start()
-        for copy in copies:
-            copy.wait()
+            if stage + 1 < count:
+                fold.reduce_copy(stage + 1).start()
+            else:
+                fold.gather_copy(fold.gather_order[0]).start()
+    for turn in range(count):
+        for fold in folds:
+            fold.gather_copy(fold.gather_order[turn]).wait()
+            if turn + 1 < count:
+                fold.gather_copy(fold.gather_order[turn + 1]).start()
 
 
 def greet(devices):
@@ -255,52 +272,174 @@
     return block // sizes[1], lax.rem(block, sizes[1])
 
 
-def halo_step(sizes, moves, listed_ref, mesh_ref, halo_ref, out, landed, send, recv):
-    place = here()
-    greet([block_at(place, sizes, move) for move in moves])
-    slots = out.shape[1]
-    own = mesh_ref.shape[0]
-    pick = one_hot(listed_ref[...], (own, listed_ref.shape[1]), 0)
-    rows = inner_rows(pick, mesh_ref[...]).astype(BF)
-    copies = []
-    for k, move in enumerate(moves):
-        out[k] = rows[k * slots : (k + 1) * slots]
-    for k, move in enumerate(moves):
-        copy = pltpu.make_async_remote_copy(
-            src_ref=out.at[k],
-            dst_ref=landed.at[k],
-            send_sem=send.at[k],
-            recv_sem=recv.at[k],
-            device_id=block_at(place, sizes, -move),
-            device_id_type=MESH,
-        )
-        copy.start()
-        copies.append(copy)
-    for copy in copies:
-        copy.wait()
-    halo_ref[...] = landed[...]
-
-
-def sum_step(bits, lo_rows, part_ref, out_ref, *refs):
+def picks(lists_ref, own):
+    _, neigh, slots = lists_ref.shape
+    listed = lists_ref[0].T
+    return jnp.concatenate(
+        [one_hot(listed[:, k : k + 1], (slots, own), 1).astype(F32) for k in range(neigh)], axis=0
+    ).astype(BF)
+
+
+def node_math(rows, summed, slope, win_ref, wout_ref, gain):
+    pre = product(rows, win_ref[0]) + product(summed, win_ref[1])
+    sig = 1.0 / (1.0 + jnp.exp(-pre))
+    hidden = (pre * sig).astype(BF)
+    normed, inverse = normalize(product(hidden, wout_ref[...]))
+    new = (rows.astype(F32) + normed * gain).astype(BF)
+    out_slope = normalize_back(slope * gain, normed, inverse).astype(BF)
+    swish = sig * (1.0 + pre * (1.0 - sig))
+    pre_slope = (outer_cols(out_slope, wout_ref[...]) * swish).astype(BF)
+    back = outer_cols(pre_slope, win_ref[1]).astype(BF)
+    direct = slope + outer_cols(pre_slope, win_ref[0])
+    return new, back, direct, slope * normed, hidden, out_slope, pre_slope
+
+
+def middle_step(
+    bits,
+    part_rows,
+    factor,
+    own_sum,
+    coarse_part,
+    mesh_ref,
+    coarse_ref,
+    grad_ref,
+    grad_coarse,
+    win_ref,
+    wout_ref,
+    gain_ref,
+    new_nodes,
+    new_coarse,
+    own_slope,
+    coarse_slope,
+    own_direct,
+    coarse_direct,
+    pack,
+    total,
+    all_rows,
+    all_sums,
+    all_hidden,
+    all_out,
+    all_pre,
+    new_send,
+    new_recv,
+    slope_send,
+    slope_recv,
+    *refs,
+):
     place = here()
     greet([across(place, bit) for bit in bits])
-    cols = part_ref.shape[1]
-    parts, lo = [], 0
-    for rows in lo_rows:
-        parts.append((part_ref, out_ref, rows, lo))
-        lo += rows
-    fold_all(make_folds(place, bits, parts, refs, cols))
+    count, kinds = len(bits), coarse_kinds(len(bits))
+    own, d = mesh_ref.shape
+    coarse = coarse_ref.shape[0]
+    folds = make_folds(place, bits, kinds, cut_parts(coarse_part, total, part_rows), refs, d, True)
+    for fold in folds:
+        fold.reduce_copy(0).start()
+    gain = gain_ref[...]
+    gains = [jnp.zeros((1, d), F32)]
+    coarse_direct[...] = jnp.zeros_like(coarse_direct)
+    pieces = 4 if own % 64 == 0 else 1
+    piece = own // pieces
+
+    def own_piece(number):
+        span = pl.ds(number * piece, piece)
+        results = node_math(
+            mesh_ref[span, :], own_sum[span, :], grad_ref[span, :].astype(F32), win_ref, wout_ref, gain
+        )
+        new_nodes[span, :], own_slope[span, :], own_direct[span, :] = results[:3]
+        gains.append(jnp.sum(results[3], axis=0, keepdims=True))
+        all_rows[span, :], all_sums[span, :] = mesh_ref[span, :], own_sum[span, :]
+        all_hidden[span, :], all_out[span, :], all_pre[span, :] = results[4:]
+
+    todo = list(range(pieces))
+    for stage in range(count):
+        if todo:
+            own_piece(todo.pop(0))
+        for fold in folds:
+            fold.reduce_copy(stage).wait()
+            fold.add(stage)
+            if stage + 1 < count:
+                fold.reduce_copy(stage + 1).start()
+            else:
+                fold.gather_copy(fold.gather_order[0]).start()
+    while todo:
+        own_piece(todo.pop(0))
+    wide = kinds.count("c")
+    for turn in range(wide):
+        for fold in folds:
+            fold.gather_copy(fold.gather_order[turn]).wait()
+            if turn + 1 < wide:
+                fold.gather_copy(fold.gather_order[turn + 1]).start()
+    spans, shares = [], []
+    for fold in folds:
+        span, _ = fold.region(fold.pending(fold.gather_order[wide]))
+        first = 1
+        for stage in range(count):
+            if kinds[stage] == "c":
+                first = first * (1 - bit_of(place, fold.order[stage]))
+        spans.append(span)
+        shares.append(jnp.full((span.size, 1), first, jnp.int32).astype(F32))
+    share = jnp.concatenate(shares, axis=0)
+    rows = jnp.concatenate([coarse_ref[span, :] for span in spans], axis=0)
+    summed = jnp.concatenate([total[span, :] for span in spans], axis=0)
+    slope = jnp.concatenate([grad_coarse[span, :] for span in spans], axis=0).astype(F32)
+    new, back, direct, gain_term, hidden, out_slope, pre_slope = node_math(
+        rows, summed, slope, win_ref, wout_ref, gain
+    )
+    direct = direct * share
+    at = 0
+    for number, (fold, span) in enumerate(zip(folds, spans)):
+        here_rows = slice(at, at + span.size)
+        new_coarse[span, :], coarse_slope[span, :] = new[here_rows], back[here_rows]
+        coarse_direct[span, :] = direct[here_rows]
+        at += span.size
+    tail = range(wide, count)
+
+    def tail_copies(number, fold, turn):
+        stage = fold.gather_order[turn]
+        return (
+            fold.gather_copy(stage, coarse_slope, (slope_send.at[number], slope_recv.at[number])),
+            fold.gather_copy(stage, new_coarse, (new_send.at[number], new_recv.at[number])),
+        )
+
+    for number, fold in enumerate(folds):
+        for copy in tail_copies(number, fold, wide):
+            copy.start()
+    span = pl.ds(own, at)
+    all_rows[span, :], all_sums[span, :] = rows, summed
+    all_hidden[span, :] = (hidden.astype(F32) * share).astype(BF)
+    all_out[span, :] = out_slope
+    all_pre[span, :] = (pre_slope.astype(F32) * share).astype(BF)
+    gains.append(jnp.sum(gain_term * share, axis=0, keepdims=True))
+    jobs = [
+        lambda: (0, inner_rows(all_rows[...], all_pre[...])),
+        lambda: (d, inner_rows(all_sums[...], all_pre[...])),
+        lambda: (2 * d, inner_rows(all_hidden[...], all_out[...])),
+    ]
+    for turn in tail:
+        if jobs:
+            lo, result = jobs.pop(0)()
+            pack[pl.ds(lo, d), :] = (result * factor).astype(BF)
+        for number, fold in enumerate(folds):
+            for copy in tail_copies(number, fold, turn):
+                copy.wait()
+            if turn + 1 < count:
+                for copy in tail_copies(number, fold, turn + 1):
+                    copy.start()
+    assert not jobs
+    rest = pack.shape[0] - 3 * d
+    pack[pl.ds(3 * d, rest), :] = jnp.broadcast_to(sum(gains) * factor, (rest, d)).astype(BF)
 
 
 def final_step(
     bits,
     sizes,
     moves,
-    lo_rows,
+    edge_cuts,
+    node_cuts,
     edge_ref,
     node_ref,
     term_ref,
-    listed_ref,
+    lists_ref,
     direct_ref,
     edge_out,
     node_out,
@@ -325,19 +464,13 @@
         copy.start()
         copies.append(copy)
     cols = edge_ref.shape[1]
-    parts, lo = [], 0
-    for rows in lo_rows:
-        parts.append((edge_ref, edge_out, rows, lo))
-        lo += rows
-    parts.append((node_ref, node_out, node_ref.shape[0], 0))
-    folds = make_folds(place, bits, parts, refs, cols)
-    fold_all(folds)
+    parts = cut_parts(edge_ref, edge_out, edge_cuts) + cut_parts(node_ref, node_out, node_cuts)
+    fold_all(make_folds(place, bits, sum_kinds(len(bits)), parts, refs, cols))
     for copy in copies:
         copy.wait()
     own = direct_ref.shape[0]
-    pick = one_hot(listed_ref[...], (own, listed_ref.shape[1]), 0)
-    back = landed[...].reshape(listed_ref.shape[1], cols)
-    nodes_grad[...] = (direct_ref[...] + product(pick, back)).astype(BF)
+    back = landed[...].reshape(landed.shape[0] * landed.shape[1], cols)
+    nodes_grad[...] = (direct_ref[...] + inner_rows(picks(lists_ref, own), back)).astype(BF)
 
 
 def edge_index(tiles_ref, own, halo):
@@ -356,11 +489,13 @@
 
 def edge_forward(
     tile_width,
+    sizes,
+    moves,
     live_ref,
     lat_ref,
     tiles_ref,
+    lists_ref,
     mesh_ref,
-    halo_ref,
     coarse_ref,
     win_ref,
     wout_ref,
@@ -372,9 +507,14 @@
     inv_ref,
     agg_own,
     agg_coarse,
+    halo_ref,
     proj_s,
     proj_r,
     agg,
+    leaving,
+    landed,
+    send,
+    recv,
 ):
     step = pl.program_id(0)
     own, halo = mesh_ref.shape[0], halo_ref.shape[0]
@@ -383,11 +523,37 @@
 
     @pl.when(step == 0)
     def _():
+        place = here()
+        greet([block_at(place, sizes, move) for move in moves])
+        slots = leaving.shape[1]
+        rows_out = product(picks(lists_ref, own), mesh_ref[...]).astype(BF)
+        copies = []
+        for k, move in enumerate(moves):
+            leaving[k] = rows_out[k * slots : (k + 1) * slots]
+        for k, move in enumerate(moves):
+            copy = pltpu.make_async_remote_copy(
+                src_ref=leaving.at[k],
+                dst_ref=landed.at[k],
+                send_sem=send.at[k],
+                recv_sem=recv.at[k],
+                device_id=block_at(place, sizes, -move),
+                device_id_type=MESH,
+            )
+            copy.start()
+            copies.append(copy)
         agg[...] = jnp.zeros_like(agg)
-        for part, lo in ((mesh_ref, 0), (halo_ref, own), (coarse_ref, own + halo)):
+
+        def project(part, lo):
             span = pl.ds(lo, part.shape[0])
-            proj_s[span, :] = product(part[...], win_ref[1]).astype(BF)
-            proj_r[span, :] = product(part[...], win_ref[2]).astype(BF)
+            proj_s[span, :] = product(part, win_ref[1]).astype(BF)
+            proj_r[span, :] = product(part, win_ref[2]).astype(BF)
+
+        project(mesh_ref[...], 0)
+        project(coarse_ref[...], own + halo)
+        for copy in copies:
+            copy.wait()
+        halo_ref[...] = landed[...].reshape(halo_ref.shape)
+        project(halo_ref[...], own)
 
     send_col, recv_col, _, recv_row = edge_index(tiles_ref, own, halo)
     rows_in = lat_ref[...]
@@ -505,67 +671,6 @@
         pack[pl.ds(4 * d + coarse, rest), :] = jnp.broadcast_to(gain_grad[...] * factor, (rest, d)).astype(BF)
 
 
-def node_step(
-    masked,
-    factor,
-    me_ref,
-    rows_ref,
-    sum_ref,
-    grad_ref,
-    win_ref,
-    wout_ref,
-    gain_ref,
-    *refs,
-):
-    if masked:
-        base, new_ref, direct_ref, agg_grad, pack, in_grad, out_grad, gain_grad = refs
-    else:
-        new_ref, direct_ref, agg_grad, in_grad, out_grad, gain_grad = refs
-
-    @pl.when(pl.program_id(0) == 0)
-    def _():
-        for acc in (in_grad, out_grad, gain_grad):
-            acc[...] = jnp.zeros_like(acc)
-
-    rows = rows_ref[...]
-    summed = sum_ref[...]
-    pre = product(rows, win_ref[0]) + product(summed, win_ref[1])
-    sig = 1.0 / (1.0 + jnp.exp(-pre))
-    hidden = (pre * sig).astype(BF)
-    normed, inverse = normalize(product(hidden, wout_ref[...]))
-    new_ref[...] = (rows.astype(F32) + normed * gain_ref[...]).astype(BF)
-    node_slope = grad_ref[...].astype(F32)
-    out_slope = normalize_back(node_slope * gain_ref[...], normed, inverse).astype(BF)
-    swish = sig * (1.0 + pre * (1.0 - sig))
-    pre_slope = (outer_cols(out_slope, wout_ref[...]) * swish).astype(BF)
-    agg_grad[...] = outer_cols(pre_slope, win_ref[1]).astype(BF)
-    direct = node_slope + outer_cols(pre_slope, win_ref[0])
-    if masked:
-        count, block = me_ref[1], rows.shape[0]
-        place = pl.program_id(0) * block + lax.broadcasted_iota(jnp.int32, (block, 1), 0)
-        share = jnp.where((place * count) // (pl.num_programs(0) * block) == me_ref[0], 1.0, 0.0)
-        direct = direct * share
-        node_slope = node_slope * share
-        hidden = (hidden.astype(F32) * share).astype(BF)
-        pre_slope = (pre_slope.astype(F32) * share).astype(BF)
-    direct_ref[...] = direct
-    gain_grad[...] += jnp.sum(node_slope * normed, axis=0, keepdims=True)
-    out_grad[...] += inner_rows(hidden, out_slope)
-    in_grad[0] += inner_rows(rows, pre_slope)
-    in_grad[1] += inner_rows(summed, pre_slope)
-    if masked:
-
-        @pl.when(pl.program_id(0) == pl.num_programs(0) - 1)
-        def _():
-            d = in_grad.shape[1]
-            for i in range(2):
-                pack[pl.ds(i * d, d), :] = ((in_grad[i] + base[pl.ds(i * d, d), :]) * factor).astype(BF)
-            pack[pl.ds(2 * d, d), :] = ((out_grad[...] + base[pl.ds(2 * d, d), :]) * factor).astype(BF)
-            rest = pack.shape[0] - 3 * d
-            gain = (gain_grad[...] + base[pl.ds(3 * d, 1), :]) * factor
-            pack[pl.ds(3 * d, rest), :] = jnp.broadcast_to(gain, (rest, d)).astype(BF)
-
-
 def whole(shape):
     zero = (0,) * len(shape)
     return pl.BlockSpec(shape, lambda i: zero)
@@ -594,31 +699,13 @@
 )
 
 
-def talking(number):
+def talking(number, grid=False):
     return pltpu.CompilerParams(
-        collective_id=number, has_side_effects=True, vmem_limit_bytes=60 * 1024 * 1024
-    )
-
-
-def node_call(me, rows, summed, grad, node_in, node_out, gain, block, factor, base=None, pack_rows=0):
-    count, d = rows.shape
-    row = by_rows(block, d)
-    masked = base is not None
-    smem = pl.BlockSpec(memory_space=pltpu.SMEM)
-    accs = [(2, d, d), (d, d), (1, d)]
-    extra_in = [whole(base.shape)] if masked else []
-    acc_specs = [whole((pack_rows, d))] if masked else [whole(shape) for shape in accs]
-    acc_shapes = [shape_of((pack_rows, d), BF)] if masked else [shape_of(shape, F32) for shape in accs]
-    return pl.pallas_call(
-        functools.partial(node_step, masked, factor),
-        grid=(count // block,),
-        in_specs=[smem, row, row, row, whole((2, d, d)), whole((d, d)), whole((1, d))] + extra_in,
-        out_specs=[row, row, row] + acc_specs,
-        out_shape=[shape_of((count, d), BF), shape_of((count, d), F32), shape_of((count, d), BF)] + acc_shapes,
-        scratch_shapes=[pltpu.VMEM(shape, F32) for shape in accs] if masked else [],
-        cost_estimate=cost(18 * count * d * d, 12 * count * d),
-        **PARAMS,
-    )(me, rows, summed, grad, node_in, node_out, gain, *([base] if masked else []))
+        collective_id=number,
+        has_side_effects=True,
+        vmem_limit_bytes=60 * 1024 * 1024,
+        dimension_semantics=("arbitrary",) if grid else None,
+    )
 
 
 def on_device(
@@ -653,61 +740,66 @@
     block = tiles * tile_width
     moves = cycle_moves(neigh, block_count)
     factor = float(edges * block_count) ** (-0.5)
-    listed = send_lists.reshape(1, halo)
-    me = jnp.stack([lax.axis_index("lat") * sizes[1] + lax.axis_index("blk"), jnp.int32(block_count)])
     e_gain, n_gain = edge_gain.reshape(1, d), node_gain.reshape(1, d)
     vmem = pl.BlockSpec(memory_space=pltpu.VMEM)
-    incoming = pl.pallas_call(
-        functools.partial(halo_step, sizes, moves),
-        in_specs=[vmem, vmem],
-        out_specs=vmem,
-        out_shape=shape_of((neigh, slots, d), BF),
-        scratch_shapes=[pltpu.VMEM((neigh, slots, d), BF)] * 2 + [pltpu.SemaphoreType.DMA((neigh,))] * 2,
-        compiler_params=talking(0),
-    )(listed, mesh_nodes).reshape(halo, d)
-
     smem = pl.BlockSpec(memory_space=pltpu.SMEM)
     wide, col = by_rows(block, d), by_rows(block, 1)
     pairs = pl.BlockSpec((tiles, 2, tile_width), lambda i: (i, 0, 0))
     tables = [whole((own, d)), whole((halo, d)), whole((coarse, d))]
     weights = [whole((3, d, d)), whole((d, d)), whole((1, d))]
-    new_edges, hidden, slope, normed, inverse, agg_own, agg_coarse = pl.pallas_call(
-        functools.partial(edge_forward, tile_width),
+    swap = [pltpu.VMEM((neigh, slots, d), BF)] * 2 + [pltpu.SemaphoreType.DMA((neigh,))] * 2
+    new_edges, hidden, slope, normed, inverse, agg_own, agg_coarse, incoming = pl.pallas_call(
+        functools.partial(edge_forward, tile_width, sizes, moves),
         grid=(edges // block,),
-        in_specs=[smem, wide, pairs] + tables + weights,
-        out_specs=[wide] * 4 + [col, whole((own, d)), whole((coarse, d))],
+        in_specs=[smem, wide, pairs, whole((1, neigh, slots)), tables[0], tables[2]] + weights,
+        out_specs=[wide] * 4 + [col, tables[0], tables[2], tables[1]],
         out_shape=[shape_of((edges, d), BF)] * 4
-        + [shape_of((edges, 1), F32), shape_of((own, d), BF), shape_of((coarse, d), BF)],
+        + [
+            shape_of((edges, 1), F32),
+            shape_of((own, d), BF),
+            shape_of((coarse, d), BF),
+            shape_of((halo, d), BF),
+        ],
         scratch_shapes=[
             pltpu.VMEM((rows, d), BF),
             pltpu.VMEM((rows, d), BF),
             pltpu.VMEM((rows, d), F32),
+        ]
+        + swap,
+        cost_estimate=cost(2 * edges * d * (3 * rows + 2 * d), 12 * edges * d),
+        compiler_params=talking(0, grid=True),
+    )(
+        tiles_live, edge_latents, edge_tiles, send_lists, mesh_nodes, coarse_nodes, edge_in, edge_out, e_gain
+    )
+    sum_rows = padded(coarse, count)
+    grown = [agg_coarse, coarse_nodes, grad_coarse]
+    if sum_rows > coarse:
+        grown = [jnp.pad(array, ((0, sum_rows - coarse), (0, 0))) for array in grown]
+    coarse_rows = split_rows(sum_rows, count, 3)
+    all_rows = own + sum_rows // 2 ** (count - 2)
+    node_rows = padded(3 * d + 1, count)
+    parts = len(coarse_rows)
+    new_nodes, new_coarse, own_slope, c_slope, own_direct, c_direct, node_pack = pl.pallas_call(
+        functools.partial(middle_step, bits, coarse_rows, factor),
+        in_specs=[vmem] * 9,
+        out_specs=[vmem] * 7,
+        out_shape=[
+            shape_of((own, d), BF),
+            shape_of((sum_rows, d), BF),
+            shape_of((own, d), BF),
+            shape_of((sum_rows, d), BF),
+            shape_of((own, d), F32),
+            shape_of((sum_rows, d), F32),
+            shape_of((node_rows, d), BF),
         ],
-        cost_estimate=cost(2 * edges * d * (3 * rows + 2 * d), 12 * edges * d),
-        **PARAMS,
-    )(tiles_live, edge_latents, edge_tiles, mesh_nodes, incoming, coarse_nodes, edge_in, edge_out, e_gain)
-    sum_rows = padded(coarse, count)
+        scratch_shapes=[pltpu.VMEM((sum_rows, d), BF)]
+        + [pltpu.VMEM((all_rows, d), BF)] * 5
+        + [pltpu.SemaphoreType.DMA((parts, count))] * 4
+        + fold_scratch(coarse_kinds(count), coarse_rows, d),
+        compiler_params=talking(1),
+    )(agg_own, grown[0], mesh_nodes, grown[1], grad_nodes, grown[2], node_in, node_out, n_gain)
     if sum_rows > coarse:
-        agg_coarse = jnp.pad(agg_coarse, ((0, sum_rows - coarse), (0, 0)))
-    coarse_rows = split_rows(sum_rows, count, 3)
-    coarse_parts = [(None, None, part, 0) for part in coarse_rows]
-    coarse_total = pl.pallas_call(
-        functools.partial(sum_step, bits, coarse_rows),
-        in_specs=[vmem],
-        out_specs=vmem,
-        out_shape=shape_of((sum_rows, d), BF),
-        scratch_shapes=fold_scratch(count, coarse_parts, d),
-        compiler_params=talking(1),
-    )(agg_coarse)[:coarse]
-    new_nodes, own_direct, own_slope, own_in, own_out, own_ngain = node_call(
-        me, mesh_nodes, agg_own, grad_nodes, node_in, node_out, n_gain, own, factor
-    )
-    base = jnp.concatenate([own_in.reshape(2 * d, d), own_out, jnp.broadcast_to(own_ngain, (8, d))], axis=0)
-    c_block = own if coarse % own == 0 else coarse
-    node_rows = padded(3 * d + 1, count)
-    new_coarse, c_direct, c_slope, node_pack = node_call(
-        me, coarse_nodes, coarse_total, grad_coarse, node_in, node_out, n_gain, c_block, factor, base, node_rows
-    )
+        new_coarse, c_slope, c_direct = (array[:coarse] for array in (new_coarse, c_slope, c_direct))
     edge_rows = padded(4 * d + coarse + 1, count)
     edges_grad, edge_pack, own_term, halo_term = pl.pallas_call(
         functools.partial(edge_backward, tile_width, factor),
@@ -735,18 +827,15 @@
         tiles_live, edge_latents, grad_edges, hidden, slope, normed, inverse, edge_tiles, mesh_nodes, incoming,
         coarse_nodes, own_slope, c_slope, own_direct, c_direct, edge_in, edge_out, e_gain,
     )
-    cuts = split_rows(edge_rows, count, 2)
-    parts = [(None, None, part, 0) for part in cuts + [node_rows]]
+    edge_cuts, node_cuts = split_rows(edge_rows, count, 6), split_rows(node_rows, count, 3)
     edge_sum, node_sum, nodes_grad = pl.pallas_call(
-        functools.partial(final_step, bits, sizes, moves, cuts),
+        functools.partial(final_step, bits, sizes, moves, edge_cuts, node_cuts),
         in_specs=[vmem] * 5,
         out_specs=[vmem] * 3,
         out_shape=[shape_of((edge_rows, d), BF), shape_of((node_rows, d), BF), shape_of((own, d), BF)],
-        scratch_shapes=[pltpu.VMEM((neigh, slots, d), BF)]
-        + [pltpu.SemaphoreType.DMA((neigh,))] * 2
-        + fold_scratch(count, parts, d),
+        scratch_shapes=swap[1:] + fold_scratch(sum_kinds(count), edge_cuts + node_cuts, d),
         compiler_params=talking(2),
-    )(edge_pack, node_pack, halo_term.reshape(neigh, slots, d), listed, own_term)
+    )(edge_pack, node_pack, halo_term.reshape(neigh, slots, d), send_lists, own_term)
     return (
         new_nodes,
         new_coarse,

time: 190 us -> 163 us (0.86)
  Pallas kernels: 173 us -> 149 us
  other arithmetic: 5.91 us -> 1.45 us
    pallas_call x6 -> x3, Pallas kernels: 148 us -> 124 us  [the longest x1 57.5 us: on_device(): pl.pallas_call(functools.partial(final_step, bits, sizes, moves, edge_cut...]
    concatenate x1 -> x0, other arithmetic: 3.87 us -> none  [on_device(): jnp.concatenate([own_in.reshape(2 * d, d), own_out, jnp.broadcast_to(own_...]
    unnamed x5 -> x14, local copies, waits for them, and re-layouts: 0.73 us -> 3.62 us
where the time goes in v1:
time: 163 us
  Pallas kernels  149 us (91%)
  local copies, waits for them, and re-layouts  10.7 us (7%)
    pallas_call x1, Pallas kernels, on_device(): pl.pallas_call(functools.partial(final_step, bits, sizes, moves, edge_cut...  57.5 us
    pallas_call x1, Pallas kernels, on_device(): pl.pallas_call(functools.partial(middle_step, bits, coarse_rows, factor),...  39.5 us
    pallas_call x1, Pallas kernels, on_device(): pl.pallas_call(functools.partial(edge_forward, tile_width, sizes, moves),...  27.4 us
    pallas_call x1, Pallas kernels, on_device(): pl.pallas_call(functools.partial(edge_backward, tile_width, factor), grid...  24.7 us
    unnamed x14, local copies, waits for them, and re-layouts  3.62 us

profile of v1, /device:TPU:0, one launch (start us, length us, event | category | flops | bytes accessed | tf_op | source)
XLA Modules:
  0.0 162.6 jit_solution(11279876973778966157)
XLA Ops:
  1.3 27.4 %shard_map.238 = (bf16[2048,512]{1,0:T(8,128)(2,1)}, bf16[2048,512]{1,0:T(8,128)(2,1)}, bf16[2048,512]{1,0:T(8,128)(2,1)}, bf16[2048,512]{1,0:T(8,128)(2,1)}, f3...) custom-call(s32[1]{0:T(128)S(6)} %copy.31.live_ref, ...), custom_call_target="tpu_custom_call" | custom-call | flops 8589934592 | bytes 12582912 | tf_op jit(solution)/shard_map/pallas_call | solution.py:751
  28.7 39.5 %shard_map.239 = (bf16[320,512]{1,0:T(8,128)(2,1)}, bf16[640,512]{1,0:T(8,128)(2,1)}, bf16[320,512]{1,0:T(8,128)(2,1)}, bf16[640,512]{1,0:T(8,128)(2,1)}, f32[32...) custom-call(bf16[320,512]{1,0:T(8,128)(2,1)} %get-tuple-element.34.own_sum, ...), custom_call_target="tpu_custom_call" | custom-call | tf_op jit(solution)/shard_map/pallas_call | solution.py:782
  68.2 24.7 %shard_map.240 = (bf16[2048,512]{1,0:T(8,128)(2,1)}, bf16[2816,512]{1,0:T(8,128)(2,1)}, f32[320,512]{1,0:T(8,128)}, bf16[64,512]{1,0:T(8,128)(2,1)}) custom-call(s32[1]{0:T(128)S(6)} %copy.31.live_ref, bf16[2048,512]{1,0:T(8,128)(2,1)} %lat_ref.3, bf16[2048,512]{1,0:T(8,128)(2,1)} %grad_ref.3, bf16[2048,512]{1,0:T(8,128)(2,1)} %get-tuple-element.39.hid_ref, ...), custom_call_target="tpu_custom_call" | custom-call | flops 10737418240 | bytes 14680064 | tf_op jit(solution)/shard_map/pallas_call | solution.py:804
  92.9 57.5 %shard_map.241 = (bf16[2816,512]{1,0:T(8,128)(2,1)}, bf16[1664,512]{1,0:T(8,128)(2,1)}, bf16[320,512]{1,0:T(8,128)(2,1)}) custom-call(bf16[2816,512]{1,0:T(8,128)(2,1)} %get-tuple-element.48.edge_ref, bf16[1664,512]{1,0:T(8,128)(2,1)} %get-tuple-element.49.node_ref, bf16[8,8,512]{2,1,0:T(8,128)(2,1)} %bitcast.9, s32[1,8,8]{2,1,0:T(8,128)} %lists_ref.3, ...), custom_call_target="tpu_custom_call" | custom-call | tf_op jit(solution)/shard_map/pallas_call | solution.py:831
  150.4 0.0 copy-start
  150.4 1.4 slice_convert_fusion
  151.9 1.9 %slice.26 = bf16[512,512]{1,0:T(8,128)(2,1)} slice(bf16[1664,512]{1,0:T(8,128)(2,1)} %get-tuple-element.55), slice={[1024:1536], [0:512]} | slice | bytes 1048576 | tf_op jit(solution)/shard_map/slice | solution.py:850
  153.7 2.3 %slice.25 = bf16[1024,512]{1,0:T(8,128)(2,1)} slice(bf16[1664,512]{1,0:T(8,128)(2,1)} %get-tuple-element.55), slice={[0:1024], [0:512]} | slice | bytes 2097152 | tf_op jit(solution)/shard_map/slice | solution.py:849
  156.0 0.0 copy-done
  156.0 0.8 slice.23
  156.8 0.0 copy-start.3
  156.8 0.9 slice.21
  157.7 0.0 copy-start.2
  157.7 0.0 copy-start.1
  157.7 1.2 slice.22
  159.0 0.0 copy-done.3
  159.0 0.7 copy.32
  159.7 0.0 copy-done.2
  159.7 0.8 copy.33
  160.5 0.0 copy-done.1
  160.5 0.0 copy-start.4
  160.5 1.3 copy.34
  161.9 0.0 copy-done.4
  161.9 0.7 copy.35
Async XLA Ops:
  150.4 5.6 %copy-start = (bf16[2816,512]{1,0:T(8,128)(2,1)S(1)}, bf16[2816,512]{1,0:T(8,128)(2,1)}, u32[]{:S(2)}) copy-start(bf16[2816,512]{1,0:T(8,128)(2,1)} %get-tuple-element.53) | copy-start | bytes 8650756
  156.8 2.1 %copy-start.3 = (bf16[320,512]{1,0:T(8,128)(2,1)S(1)}, bf16[320,512]{1,0:T(8,128)(2,1)}, u32[]{:S(2)}) copy-start(bf16[320,512]{1,0:T(8,128)(2,1)} %get-tuple-element.70) | copy-start | bytes 983044
  157.7 2.0 %copy-start.2 = (bf16[640,512]{1,0:T(8,128)(2,1)S(1)}, bf16[640,512]{1,0:T(8,128)(2,1)}, u32[]{:S(2)}) copy-start(bf16[640,512]{1,0:T(8,128)(2,1)} %get-tuple-element.71) | copy-start | bytes 1966084
  157.7 2.8 %copy-start.1 = (bf16[2048,512]{1,0:T(8,128)(2,1)S(1)}, bf16[2048,512]{1,0:T(8,128)(2,1)}, u32[]{:S(2)}) copy-start(bf16[2048,512]{1,0:T(8,128)(2,1)} %get-tuple-element.72) | copy-start | bytes 6291460
  160.5 1.3 copy-start.4

commit v2 on v1

--- a/solution.py
+++ b/solution.py
@@ -95,7 +95,8 @@
         self.source, self.target, self.lo = source, target, lo
         self.rows, self.cols = rows, cols
         self.arrive, self.held = refs[:count], refs[count : 2 * count - 1]
-        self.rs_send, self.rs_recv, self.ag_send, self.ag_recv = refs[2 * count - 1 : 2 * count + 3]
+        if refs:
+            self.rs_send, self.rs_recv, self.ag_send, self.ag_recv = refs[2 * count - 1 :]
         self.sizes = Fold.shapes(kinds, rows, cols)
         self.gather_order = list(reversed(range(count)))
         if wide_first:
@@ -197,6 +198,30 @@
         )
 
 
+    def delivery(self):
+        span = pl.ds(self.lo, self.rows)
+        return pltpu.make_async_copy(self.target.at[span, :], self.out.at[span, :], self.out_sem)
+
+    def deliver(self):
+        self.delivery().start()
+
+    def begin(self, turn):
+        count = len(self.order)
+        if turn < count:
+            self.reduce_copy(turn).start()
+        elif turn < 2 * count:
+            self.gather_copy(self.gather_order[turn - count]).start()
+
+    def advance(self, turn):
+        count = len(self.order)
+        if turn < count:
+            self.reduce_copy(turn).wait()
+            self.add(turn)
+        else:
+            self.gather_copy(self.gather_order[turn - count]).wait()
+        self.begin(turn + 1)
+
+
 def sum_kinds(count):
     return ["c", "c"] + ["r"] * (count - 2)
 
@@ -216,7 +241,8 @@
     count, folds = len(bits), []
     for number, (source, target, rows, lo) in enumerate(parts):
         mine, refs = refs[: 2 * count + 3], refs[2 * count + 3 :]
-        folds.append(Fold(place, turned(bits, number), kinds, source, target, lo, rows, cols, mine, wide_first))
+        order = turned(bits, number)
+        folds.append(Fold(place, order, kinds, source, target, lo, rows, cols, mine, wide_first))
     return folds
 
 
@@ -226,25 +252,6 @@
         parts.append((source, target, rows, lo))
         lo += rows
     return parts
-
-
-def fold_all(folds):
-    count = len(folds[0].order)
-    for fold in folds:
-        fold.reduce_copy(0).start()
-    for stage in range(count):
-        for fold in folds:
-            fold.reduce_copy(stage).wait()
-            fold.add(stage)
-            if stage + 1 < count:
-                fold.reduce_copy(stage + 1).start()
-            else:
-                fold.gather_copy(fold.gather_order[0]).start()
-    for turn in range(count):
-        for fold in folds:
-            fold.gather_copy(fold.gather_order[turn]).wait()
-            if turn + 1 < count:
-                fold.gather_copy(fold.gather_order[turn + 1]).start()
 
 
 def greet(devices):
@@ -308,20 +315,19 @@
     wout_ref,
     gain_ref,
     new_nodes,
-    new_coarse,
+    new_part,
     own_slope,
     coarse_slope,
     own_direct,
-    coarse_direct,
+    direct_part,
     pack,
+    node_gain,
     total,
     all_rows,
     all_sums,
     all_hidden,
     all_out,
     all_pre,
-    new_send,
-    new_recv,
     slope_send,
     slope_recv,
     *refs,
@@ -336,7 +342,6 @@
         fold.reduce_copy(0).start()
     gain = gain_ref[...]
     gains = [jnp.zeros((1, d), F32)]
-    coarse_direct[...] = jnp.zeros_like(coarse_direct)
     pieces = 4 if own % 64 == 0 else 1
     piece = own // pieces
 
@@ -385,25 +390,20 @@
     new, back, direct, gain_term, hidden, out_slope, pre_slope = node_math(
         rows, summed, slope, win_ref, wout_ref, gain
     )
-    direct = direct * share
+    new_part[...] = new
+    direct_part[...] = direct * share
     at = 0
-    for number, (fold, span) in enumerate(zip(folds, spans)):
-        here_rows = slice(at, at + span.size)
-        new_coarse[span, :], coarse_slope[span, :] = new[here_rows], back[here_rows]
-        coarse_direct[span, :] = direct[here_rows]
+    for fold, span in zip(folds, spans):
+        coarse_slope[span, :] = back[at : at + span.size]
         at += span.size
     tail = range(wide, count)
 
-    def tail_copies(number, fold, turn):
+    def tail_copy(number, fold, turn):
         stage = fold.gather_order[turn]
-        return (
-            fold.gather_copy(stage, coarse_slope, (slope_send.at[number], slope_recv.at[number])),
-            fold.gather_copy(stage, new_coarse, (new_send.at[number], new_recv.at[number])),
-        )
+        return fold.gather_copy(stage, coarse_slope, (slope_send.at[number], slope_recv.at[number]))
 
     for number, fold in enumerate(folds):
-        for copy in tail_copies(number, fold, wide):
-            copy.start()
+        tail_copy(number, fold, wide).start()
     span = pl.ds(own, at)
     all_rows[span, :], all_sums[span, :] = rows, summed
     all_hidden[span, :] = (hidden.astype(F32) * share).astype(BF)
@@ -420,57 +420,11 @@
             lo, result = jobs.pop(0)()
             pack[pl.ds(lo, d), :] = (result * factor).astype(BF)
         for number, fold in enumerate(folds):
-            for copy in tail_copies(number, fold, turn):
-                copy.wait()
+            tail_copy(number, fold, turn).wait()
             if turn + 1 < count:
-                for copy in tail_copies(number, fold, turn + 1):
-                    copy.start()
+                tail_copy(number, fold, turn + 1).start()
     assert not jobs
-    rest = pack.shape[0] - 3 * d
-    pack[pl.ds(3 * d, rest), :] = jnp.broadcast_to(sum(gains) * factor, (rest, d)).astype(BF)
-
-
-def final_step(
-    bits,
-    sizes,
-    moves,
-    edge_cuts,
-    node_cuts,
-    edge_ref,
-    node_ref,
-    term_ref,
-    lists_ref,
-    direct_ref,
-    edge_out,
-    node_out,
-    nodes_grad,
-    landed,
-    send,
-    recv,
-    *refs,
-):
-    place = here()
-    greet([across(place, bit) for bit in bits] + [block_at(place, sizes, -move) for move in moves])
-    copies = []
-    for k, move in enumerate(moves):
-        copy = pltpu.make_async_remote_copy(
-            src_ref=term_ref.at[k],
-            dst_ref=landed.at[k],
-            send_sem=send.at[k],
-            recv_sem=recv.at[k],
-            device_id=block_at(place, sizes, move),
-            device_id_type=MESH,
-        )
-        copy.start()
-        copies.append(copy)
-    cols = edge_ref.shape[1]
-    parts = cut_parts(edge_ref, edge_out, edge_cuts) + cut_parts(node_ref, node_out, node_cuts)
-    fold_all(make_folds(place, bits, sum_kinds(len(bits)), parts, refs, cols))
-    for copy in copies:
-        copy.wait()
-    own = direct_ref.shape[0]
-    back = landed[...].reshape(landed.shape[0] * landed.shape[1], cols)
-    nodes_grad[...] = (direct_ref[...] + inner_rows(picks(lists_ref, own), back)).astype(BF)
+    node_gain[...] = sum(gains)
 
 
 def edge_index(tiles_ref, own, halo):
@@ -584,6 +538,13 @@
 def edge_backward(
     tile_width,
     factor,
+    bits,
+    sizes,
+    moves,
+    steps,
+    node_cuts,
+    edge_cuts,
+    coarse_cuts,
     live_ref,
     lat_ref,
     grad_ref,
@@ -598,77 +559,308 @@
     own_slope,
     coarse_slope,
     own_direct,
-    coarse_direct,
+    direct_part,
+    new_part,
+    node_pack,
+    node_gain,
+    lists_ref,
     win_ref,
     wout_ref,
     gain_ref,
     edges_grad,
-    pack,
-    own_term,
-    halo_term,
-    table,
+    edge_out,
+    node_out,
+    coarse_out,
+    nodes_grad,
+    edge_sum,
+    node_sum,
+    new_coarse,
+    out_sems,
+    coarse_sem,
+    slots_table,
     sent,
     received,
     first_acc,
     out_acc,
-    gain_grad,
+    gain_acc,
+    pre_all,
+    pack,
+    leaving,
+    landed,
+    send,
+    recv,
+    new_send,
+    new_recv,
+    *refs,
 ):
     step = pl.program_id(0)
     own, halo = mesh_ref.shape[0], halo_ref.shape[0]
-    rows = table.shape[0]
+    rows, d = slots_table.shape
     block = lat_ref.shape[0]
+    coarse = coarse_ref.shape[0]
+    place, count = here(), len(bits)
+    kinds = sum_kinds(count)
+    each = 2 * count + 3
+    nodes = make_folds(place, bits, kinds, cut_parts(node_pack, node_sum, node_cuts), refs, d)
+    refs = refs[each * len(nodes) :]
+    groups, lo = [], 0
+    for cuts in edge_cuts:
+        group = []
+        for size in cuts:
+            group.append((pack, edge_sum, size, lo))
+            lo += size
+        groups.append(group)
+    flat = make_folds(place, bits, kinds, [part for group in groups for part in group], refs, d)
+    edges = []
+    for group in groups:
+        edges.append(flat[: len(group)])
+        flat = flat[len(group) :]
+    for number, fold in enumerate(nodes + [fold for group in edges for fold in group]):
+        fold.out, fold.out_sem = (node_out if number < len(nodes) else edge_out), out_sems.at[number]
+    shares = [
+        Fold(place, turned(bits, number), coarse_kinds(count), None, target, lo, size, d, (), True)
+        for number, (_, target, size, lo) in enumerate(cut_parts(None, new_coarse, coarse_cuts))
+    ]
+    wide = coarse_kinds(count).count("c")
+    spans = [fold.region(fold.pending(fold.gather_order[wide]))[0] for fold in shares]
+
+    def share_copy(number, turn):
+        fold = shares[number]
+        stage = fold.gather_order[turn]
+        return fold.gather_copy(stage, new_coarse, (new_send.at[number], new_recv.at[number]))
+
+    groups = {"n": nodes, "a": edges[0] + edges[1], "b": edges[4], "c": edges[2], "d": edges[3]}
+    turns = {name: 0 for name in groups}
+
+    def move(names):
+        for name in names:
+            if turns[name] < 2 * count:
+                for fold in groups[name]:
+                    fold.advance(turns[name])
+                    if turns[name] == 2 * count - 1:
+                        fold.deliver()
+                turns[name] += 1
+            if name == "n" and wide + turns["n"] <= count:
+                for number in range(len(shares)):
+                    share_copy(number, wide + turns["n"] - 1).wait()
+                    if wide + turns["n"] < count:
+                        share_copy(number, wide + turns["n"]).start()
+
+    table = {0: "n", 2: "n", 3: "n", 5: "na", 7: "na", 8: "b", 9: "a", 10: "nb", 11: "a", 12: "nabcd", 13: "nabcd",
+             14: "nabcd", 15: "nabcd"}
 
     @pl.when(step == 0)
     def _():
-        for acc in (sent, received, first_acc, out_acc, gain_grad):
+        greet([across(place, bit) for bit in bits] + [block_at(place, sizes, -move) for move in moves])
+        for fold in nodes:
+            fold.begin(0)
+        at = 0
+        for number, span in enumerate(spans):
+            new_coarse[span, :] = new_part[pl.ds(at, span.size), :]
+            at += span.size
+            share_copy(number, wide).start()
+        for acc in (sent, received, first_acc, out_acc, gain_acc):
             acc[...] = jnp.zeros_like(acc)
-        table[pl.ds(0, own), :] = own_slope[...]
-        table[pl.ds(own, halo), :] = jnp.zeros((halo, table.shape[1]), BF)
-        table[pl.ds(own + halo, rows - own - halo), :] = coarse_slope[...]
-
-    _, recv_col, send_row, recv_row = edge_index(tiles_ref, own, halo)
-    place = step * block + lax.broadcasted_iota(jnp.int32, (block, 1), 0)
-    alive = jnp.where(place < live_ref[0] * tile_width, 1.0, 0.0)
-    edge_slope = grad_ref[...].astype(F32)
-    message_slope = (
-        edge_slope + product(one_hot(recv_col, (block, rows), 1), table[...])
-    ) * alive
-    normed = norm_ref[...].astype(F32)
-    gain_grad[...] += jnp.sum(message_slope * normed, axis=0, keepdims=True)
-    out_slope = normalize_back(message_slope * gain_ref[...], normed, inv_ref[...]).astype(BF)
-    out_acc[...] += inner_rows(hid_ref[...], out_slope)
-    pre_slope = (outer_cols(out_slope, wout_ref[...]) * slope_ref[...].astype(F32)).astype(BF)
-    edges_grad[...] = (edge_slope + outer_cols(pre_slope, win_ref[0])).astype(BF)
-    first_acc[...] += inner_rows(lat_ref[...], pre_slope)
-    sent[...] += product(one_hot(send_row, (rows, block), 0), pre_slope)
-    received[...] += product(one_hot(recv_row, (rows, block), 0), pre_slope)
-
-    @pl.when(step == pl.num_programs(0) - 1)
+        slots_table[pl.ds(0, own), :] = own_slope[...]
+        slots_table[pl.ds(own, halo), :] = jnp.zeros((halo, d), BF)
+        slots_table[pl.ds(own + halo, coarse), :] = coarse_slope[...]
+
+    @pl.when(step < steps)
     def _():
-        d = first_acc.shape[0]
-        coarse = coarse_ref.shape[0]
-        pack[pl.ds(0, d), :] = (first_acc[...] * factor).astype(BF)
-        pack[pl.ds(3 * d, d), :] = (out_acc[...] * factor).astype(BF)
-        sums = [None, None]
+        _, recv_col, _, _ = edge_index(tiles_ref, own, halo)
+        at_row = step * block + lax.broadcasted_iota(jnp.int32, (block, 1), 0)
+        alive = jnp.where(at_row < live_ref[0] * tile_width, 1.0, 0.0)
+        edge_slope = grad_ref[...].astype(F32)
+        message_slope = (
+            edge_slope + product(one_hot(recv_col, (block, rows), 1), slots_table[...])
+        ) * alive
+        normed = norm_ref[...].astype(F32)
+        gain_acc[...] += jnp.sum(message_slope * normed, axis=0, keepdims=True)
+        out_slope = normalize_back(message_slope * gain_ref[...], normed, inv_ref[...]).astype(BF)
+        out_acc[...] += inner_rows(hid_ref[...], out_slope)
+        pre_slope = (outer_cols(out_slope, wout_ref[...]) * slope_ref[...].astype(F32)).astype(BF)
+        pre_all[pl.ds(pl.multiple_of(step * block, block), block), :] = pre_slope
+        first_acc[...] += inner_rows(lat_ref[...], pre_slope)
+
+    starts = [group[0].lo for group in edges]
+
+    @pl.when(step == steps - 1)
+    def _():
+        pack[pl.ds(starts[0], d), :] = (first_acc[...] * factor).astype(BF)
+        pack[pl.ds(starts[1], d), :] = (out_acc[...] * factor).astype(BF)
+        for fold in groups["a"]:
+            fold.begin(0)
+
+    def scatter(kind, total):
+        row = edge_index(tiles_ref, own, halo)[kind]
+        at_block = pl.ds(pl.multiple_of(lax.rem(step, steps) * block, block), block)
+        total[...] += product(one_hot(row, (rows, block), 0), pre_all[at_block, :])
+
+    def weight_of(source):
+        weight = None
         for part, lo in ((mesh_ref, 0), (halo_ref, own), (coarse_ref, own + halo)):
-            span = pl.ds(lo, part.shape[0])
-            total = None
-            for which, source in enumerate((sent, received)):
-                piece = source[span, :].astype(BF)
-                weight = inner_rows(part[...], piece)
-                sums[which] = weight if sums[which] is None else sums[which] + weight
-                back = outer_cols(piece, win_ref[1 + which])
-                total = back if total is None else total + back
-            if part is mesh_ref:
-                own_term[...] = total + own_direct[...]
-            elif part is halo_ref:
-                halo_term[...] = total.astype(BF)
-            else:
-                pack[pl.ds(4 * d, coarse), :] = (total + coarse_direct[...]).astype(BF)
-        pack[pl.ds(d, d), :] = (sums[0] * factor).astype(BF)
-        pack[pl.ds(2 * d, d), :] = (sums[1] * factor).astype(BF)
-        rest = pack.shape[0] - 4 * d - coarse
-        pack[pl.ds(4 * d + coarse, rest), :] = jnp.broadcast_to(gain_grad[...] * factor, (rest, d)).astype(BF)
+            term = inner_rows(part[...], source[pl.ds(lo, part.shape[0]), :].astype(BF))
+            weight = term if weight is None else weight + term
+        return (weight * factor).astype(BF)
+
+    def back(lo, size):
+        span = pl.ds(lo, size)
+        return outer_cols(sent[span, :].astype(BF), win_ref[1]) + outer_cols(
+            received[span, :].astype(BF), win_ref[2]
+        )
+
+    @pl.when(step // steps == 1)
+    def _():
+        scatter(3, received)
+
+    @pl.when(step == 2 * steps - 1)
+    def _():
+        pack[pl.ds(starts[4], d), :] = weight_of(received)
+        for fold in groups["b"]:
+            fold.begin(0)
+
+    @pl.when(step // steps == 2)
+    def _():
+        scatter(2, sent)
+
+    slots = leaving.shape[1]
+
+    def home_copy(k):
+        return pltpu.make_async_remote_copy(
+            src_ref=leaving.at[k],
+            dst_ref=landed.at[k],
+            send_sem=send.at[k],
+            recv_sem=recv.at[k],
+            device_id=block_at(place, sizes, moves[k]),
+            device_id_type=MESH,
+        )
+
+    @pl.when(step == 3 * steps - 1)
+    def _():
+        pack[pl.ds(starts[2], coarse), :] = back(own + halo, coarse).astype(BF)
+        at = 0
+        for fold, span in zip(shares, spans):
+            here_span = pl.ds(pl.multiple_of(starts[2] + span.start, 16), span.size)
+            pack[here_span, :] = (
+                pack[here_span, :].astype(F32) + direct_part[pl.ds(at, span.size), :]
+            ).astype(BF)
+            at += span.size
+        rest = starts[3] - starts[2] - coarse
+        which = lax.broadcasted_iota(jnp.int32, (rest, d), 0)
+        pack[pl.ds(starts[2] + coarse, rest), :] = (
+            jnp.where(which == 0, gain_acc[...], node_gain[...]) * factor
+        ).astype(BF)
+        for fold in groups["c"]:
+            fold.begin(0)
+        pack[pl.ds(starts[3], d), :] = weight_of(sent)
+        for fold in groups["d"]:
+            fold.begin(0)
+        leave = back(own, halo).astype(BF)
+        for k in range(len(moves)):
+            leaving[k] = leave[k * slots : (k + 1) * slots]
+        for k in range(len(moves)):
+            home_copy(k).start()
+
+    @pl.when(step // steps == 3)
+    def _():
+        at_block = pl.ds(pl.multiple_of((step - 3 * steps) * block, block), block)
+        edges_grad[...] = (grad_ref[...].astype(F32) + outer_cols(pre_all[at_block, :], win_ref[0])).astype(BF)
+
+    for part, names in table.items():
+
+        @pl.when(step == part * 4 * steps // 16)
+        def _():
+            move(names)
+
+    @pl.when(step == 4 * steps - 1)
+    def _():
+        direct = own_direct[...] + back(0, own)
+        whole_coarse = pltpu.make_async_copy(new_coarse, coarse_out, coarse_sem)
+        while wide + turns["n"] <= count:
+            move("n")
+        whole_coarse.start()
+        while any(turn < 2 * count for turn in turns.values()):
+            move("nabcd")
+        for k in range(len(moves)):
+            home_copy(k).wait()
+        home = landed[...].reshape(halo, d)
+        nodes_grad[...] = (direct + inner_rows(picks(lists_ref, own), home)).astype(BF)
+        for name in groups:
+            for fold in groups[name]:
+                fold.delivery().wait()
+        whole_coarse.wait()
+
+
+def hand_out(
+    starts,
+    coarse,
+    edge_sum,
+    node_sum,
+    new_coarse,
+    nodes_grad,
+    new_nodes,
+    new_edges,
+    edges_grad,
+    edge_in,
+    edge_out,
+    coarse_grad,
+    node_in,
+    node_out,
+    coarse_new,
+    mesh_grad,
+    mesh_new,
+    edges_new,
+    edges_back,
+    edge_gain,
+    node_gain,
+    held,
+    tail,
+    come,
+    leave,
+    tail_sem,
+):
+    d = edge_sum.shape[1]
+    last = pltpu.make_async_copy(edge_sum.at[pl.ds(starts[2] + coarse, tail.shape[0])], tail, tail_sem)
+    last.start()
+    jobs = hand_jobs(
+        starts, coarse, edge_sum, node_sum, new_coarse, nodes_grad, new_nodes, new_edges, edges_grad, edge_in,
+        edge_out, coarse_grad, node_in, node_out, coarse_new, mesh_grad, mesh_new, edges_new, edges_back,
+    )
+    moved, at = [], 0
+    for number, (source, lo, target, target_lo, size) in enumerate(jobs):
+        here_span = held.at[pl.ds(at, size)]
+        at += size
+        moved.append(
+            (
+                pltpu.make_async_copy(source.at[pl.ds(lo, size)], here_span, come.at[number]),
+                pltpu.make_async_copy(here_span, target.at[pl.ds(target_lo, size)], leave.at[number]),
+            )
+        )
+    for first, _ in moved:
+        first.start()
+    for first, second in moved:
+        first.wait()
+        second.start()
+    last.wait()
+    edge_gain[...] = tail[pl.ds(0, 1), :].astype(F32)
+    node_gain[...] = tail[pl.ds(1, 1), :].astype(F32)
+    for _, second in moved:
+        second.wait()
+
+
+def hand_jobs(
+    starts, coarse, edge_sum, node_sum, new_coarse, nodes_grad, new_nodes, new_edges, edges_grad, edge_in,
+    edge_out, coarse_grad, node_in, node_out, coarse_new, mesh_grad, mesh_new, edges_new, edges_back,
+):
+    d, own, edges = edge_sum.shape[1], new_nodes.shape[0], new_edges.shape[0]
+    jobs = []
+    for source, target in ((new_edges, edges_new), (edges_grad, edges_back)):
+        jobs += [(source, lo, target, lo, d) for lo in range(0, edges, d)]
+    jobs += [(node_sum, 0, node_in, 0, d), (node_sum, d, node_in, d, d), (node_sum, 2 * d, node_out, 0, d)]
+    jobs += [(new_coarse, 0, coarse_new, 0, coarse), (new_nodes, 0, mesh_new, 0, own)]
+    jobs += [(edge_sum, starts[0], edge_in, 0, d), (edge_sum, starts[3], edge_in, d, d)]
+    jobs += [(edge_sum, starts[4], edge_in, 2 * d, d), (edge_sum, starts[1], edge_out, 0, d)]
+    return jobs + [(edge_sum, starts[2], coarse_grad, 0, coarse), (nodes_grad, 0, mesh_grad, 0, own)]
 
 
 def whole(shape):
@@ -776,79 +968,141 @@
     if sum_rows > coarse:
         grown = [jnp.pad(array, ((0, sum_rows - coarse), (0, 0))) for array in grown]
     coarse_rows = split_rows(sum_rows, count, 3)
-    all_rows = own + sum_rows // 2 ** (count - 2)
-    node_rows = padded(3 * d + 1, count)
+    share_rows = sum_rows // 2 ** (count - 2)
+    all_rows = own + share_rows
+    node_rows = padded(3 * d, count)
     parts = len(coarse_rows)
-    new_nodes, new_coarse, own_slope, c_slope, own_direct, c_direct, node_pack = pl.pallas_call(
+    new_nodes, new_part, own_slope, c_slope, own_direct, direct_part, node_pack, node_gain_part = pl.pallas_call(
         functools.partial(middle_step, bits, coarse_rows, factor),
         in_specs=[vmem] * 9,
-        out_specs=[vmem] * 7,
+        out_specs=[vmem] * 8,
         out_shape=[
             shape_of((own, d), BF),
-            shape_of((sum_rows, d), BF),
+            shape_of((share_rows, d), BF),
             shape_of((own, d), BF),
             shape_of((sum_rows, d), BF),
             shape_of((own, d), F32),
-            shape_of((sum_rows, d), F32),
+            shape_of((share_rows, d), F32),
             shape_of((node_rows, d), BF),
+            shape_of((1, d), F32),
         ],
         scratch_shapes=[pltpu.VMEM((sum_rows, d), BF)]
         + [pltpu.VMEM((all_rows, d), BF)] * 5
-        + [pltpu.SemaphoreType.DMA((parts, count))] * 4
+        + [pltpu.SemaphoreType.DMA((parts, count))] * 2
         + fold_scratch(coarse_kinds(count), coarse_rows, d),
         compiler_params=talking(1),
     )(agg_own, grown[0], mesh_nodes, grown[1], grad_nodes, grown[2], node_in, node_out, n_gain)
     if sum_rows > coarse:
-        new_coarse, c_slope, c_direct = (array[:coarse] for array in (new_coarse, c_slope, c_direct))
-    edge_rows = padded(4 * d + coarse + 1, count)
-    edges_grad, edge_pack, own_term, halo_term = pl.pallas_call(
-        functools.partial(edge_backward, tile_width, factor),
-        grid=(edges // block,),
-        in_specs=[smem] + [wide] * 5 + [col, pairs] + tables
-        + [whole((own, d)), whole((coarse, d))] * 2 + weights,
-        out_specs=[wide, whole((edge_rows, d)), whole((own, d)), whole((halo, d))],
+        c_slope = c_slope[:coarse]
+    sections = [d, d, coarse + 2, d, d]
+    edge_cuts = [split_rows(section, count, 2) for section in sections]
+    node_cuts = split_rows(node_rows, count, 3)
+    starts = [sum(sum(cuts) for cuts in edge_cuts[:i]) for i in range(len(sections))]
+    edge_rows = sum(sum(cuts) for cuts in edge_cuts)
+    steps = edges // block
+
+    away = pl.BlockSpec(memory_space=pl.ANY)
+    cuts = node_cuts + [size for section in edge_cuts for size in section]
+
+    def once(width):
+        return pl.BlockSpec((block, width), lambda i: (i - ((i // steps + 3) // 4) * (i - (steps - 1)), 0))
+
+    again = pl.BlockSpec((block, d), lambda i: (lax.rem(i, steps), 0))
+    again_pairs = pl.BlockSpec((tiles, 2, tile_width), lambda i: (lax.rem(i, steps), 0, 0))
+    later = pl.BlockSpec((block, d), lambda i: ((i // (3 * steps)) * (i - 3 * steps), 0))
+    edges_grad, edge_sum, node_sum, new_coarse, nodes_grad = pl.pallas_call(
+        functools.partial(
+            edge_backward, tile_width, factor, bits, sizes, moves, steps, node_cuts, edge_cuts, coarse_rows
+        ),
+        grid=(4 * steps,),
+        in_specs=[smem, once(d), again] + [once(d)] * 3 + [once(1), again_pairs] + [vmem] * 14,
+        out_specs=[later] + [away] * 3 + [vmem],
         out_shape=[
             shape_of((edges, d), BF),
             shape_of((edge_rows, d), BF),
-            shape_of((own, d), F32),
-            shape_of((halo, d), BF),
+            shape_of((node_rows, d), BF),
+            shape_of((sum_rows, d), BF),
+            shape_of((own, d), BF),
         ],
         scratch_shapes=[
+            pltpu.VMEM((edge_rows, d), BF),
+            pltpu.VMEM((node_rows, d), BF),
+            pltpu.VMEM((sum_rows, d), BF),
+            pltpu.SemaphoreType.DMA((len(cuts),)),
+            pltpu.SemaphoreType.DMA,
             pltpu.VMEM((rows, d), BF),
             pltpu.VMEM((rows, d), F32),
             pltpu.VMEM((rows, d), F32),
             pltpu.VMEM((d, d), F32),
             pltpu.VMEM((d, d), F32),
             pltpu.VMEM((1, d), F32),
-        ],
+            pltpu.VMEM((edges, d), BF),
+            pltpu.VMEM((edge_rows, d), BF),
+        ]
+        + swap
+        + [pltpu.SemaphoreType.DMA((parts, count))] * 2
+        + fold_scratch(sum_kinds(count), cuts, d),
         cost_estimate=cost(2 * edges * d * (3 * rows + 4 * d), 14 * edges * d),
-        **PARAMS,
+        compiler_params=talking(2, grid=True),
     )(
         tiles_live, edge_latents, grad_edges, hidden, slope, normed, inverse, edge_tiles, mesh_nodes, incoming,
-        coarse_nodes, own_slope, c_slope, own_direct, c_direct, edge_in, edge_out, e_gain,
+        coarse_nodes, own_slope, c_slope, own_direct, direct_part, new_part, node_pack, node_gain_part, send_lists,
+        edge_in, edge_out, e_gain,
     )
-    edge_cuts, node_cuts = split_rows(edge_rows, count, 6), split_rows(node_rows, count, 3)
-    edge_sum, node_sum, nodes_grad = pl.pallas_call(
-        functools.partial(final_step, bits, sizes, moves, edge_cuts, node_cuts),
-        in_specs=[vmem] * 5,
-        out_specs=[vmem] * 3,
-        out_shape=[shape_of((edge_rows, d), BF), shape_of((node_rows, d), BF), shape_of((own, d), BF)],
-        scratch_shapes=swap[1:] + fold_scratch(sum_kinds(count), edge_cuts + node_cuts, d),
-        compiler_params=talking(2),
-    )(edge_pack, node_pack, halo_term.reshape(neigh, slots, d), send_lists, own_term)
+    sources = [edge_sum, node_sum, new_coarse, nodes_grad, new_nodes, new_edges, edges_grad]
+    results = [
+        shape_of((3 * d, d), BF),
+        shape_of((d, d), BF),
+        shape_of((coarse, d), BF),
+        shape_of((2 * d, d), BF),
+        shape_of((d, d), BF),
+        shape_of((coarse, d), BF),
+        shape_of((own, d), BF),
+        shape_of((own, d), BF),
+        shape_of((edges, d), BF),
+        shape_of((edges, d), BF),
+    ]
+    jobs = hand_jobs(starts, coarse, *sources, *results)
+    (
+        g_in,
+        g_out,
+        coarse_grad,
+        n_in,
+        n_out,
+        coarse_new,
+        mesh_grad,
+        mesh_new,
+        new_edges,
+        edges_grad,
+        edge_gain_grad,
+        node_gain_grad,
+    ) = pl.pallas_call(
+        functools.partial(hand_out, starts, coarse),
+        in_specs=[away] * len(sources),
+        out_specs=[away] * len(results) + [vmem] * 2,
+        out_shape=results + [shape_of((1, d), F32)] * 2,
+        scratch_shapes=[
+            pltpu.VMEM((sum(job[-1] for job in jobs), d), BF),
+            pltpu.VMEM((16, d), BF),
+            pltpu.SemaphoreType.DMA((len(jobs),)),
+            pltpu.SemaphoreType.DMA((len(jobs),)),
+            pltpu.SemaphoreType.DMA,
+        ],
+        compiler_params=pltpu.CompilerParams(vmem_limit_bytes=60 * 1024 * 1024),
+    )(*sources)
     return (
-        new_nodes,
-        new_coarse,
+        mesh_new,
+        coarse_new,
         new_edges,
-        nodes_grad,
-        edge_sum[4 * d : 4 * d + coarse],
+        mesh_grad,
+        coarse_grad,
         edges_grad,
-        edge_sum[: 3 * d].reshape(3, d, d),
-        edge_sum[3 * d : 4 * d],
-        edge_sum[4 * d + coarse].astype(F32),
-        node_sum[: 2 * d].reshape(2, d, d),
-        node_sum[2 * d : 3 * d],
-        node_sum[3 * d].astype(F32),
+        g_in.reshape(3, d, d),
+        g_out,
+        edge_gain_grad[0],
+        n_in.reshape(2, d, d),
+        n_out,
+        node_gain_grad[0],
     )
 
 

time: 163 us -> 150 us (0.920)
  local copies, waits for them, and re-layouts: 10.7 us -> 0 us
    slice x5 -> x0, local copies, waits for them, and re-layouts: 7.08 us -> none  [the longest x1 2.26 us: on_device(): node_sum[:2 * d].reshape(2, d, d)]
    pallas_call x1, Pallas kernels: 39.5 us -> 35.3 us  [on_device(): pl.pallas_call(functools.partial(middle_step, bits, coarse_rows, factor),...]
    unnamed x14 -> x0, local copies, waits for them, and re-layouts: 3.62 us -> none
    pallas_call x2, Pallas kernels: 82.2 us -> 85.6 us  [the longest x1 77.3 us: on_device(): pl.pallas_call(functools.partial(edge_backward, tile_width, factor, bits,...]
where the time goes in v2:
time: 150 us
  Pallas kernels  148 us (99%)
    pallas_call x1, Pallas kernels, on_device(): pl.pallas_call(functools.partial(edge_backward, tile_width, factor, bits,...  77.3 us
    pallas_call x1, Pallas kernels, on_device(): pl.pallas_call(functools.partial(middle_step, bits, coarse_rows, factor),...  35.3 us
    pallas_call x1, Pallas kernels, on_device(): pl.pallas_call(functools.partial(edge_forward, tile_width, sizes, moves),...  27.4 us
    pallas_call x1, Pallas kernels, on_device(): pl.pallas_call(functools.partial(hand_out, starts, coarse), in_specs=[awa...  8.31 us

profile of v2, /device:TPU:0, one launch (start us, length us, event | category | flops | bytes accessed | tf_op | source)
XLA Modules:
  0.0 149.8 jit_solution(15466903493800159747)
XLA Ops:
  1.3 27.4 %shard_map.238 = (bf16[2048,512]{1,0:T(8,128)(2,1)}, bf16[2048,512]{1,0:T(8,128)(2,1)}, bf16[2048,512]{1,0:T(8,128)(2,1)}, bf16[2048,512]{1,0:T(8,128)(2,1)}, f3...) custom-call(s32[1]{0:T(128)S(6)} %copy.27.live_ref, ...), custom_call_target="tpu_custom_call" | custom-call | flops 8589934592 | bytes 12582912 | tf_op jit(solution)/shard_map/pallas_call | solution.py:943
  28.7 35.3 %shard_map.239 = (bf16[320,512]{1,0:T(8,128)(2,1)}, bf16[80,512]{1,0:T(8,128)(2,1)}, bf16[320,512]{1,0:T(8,128)(2,1)}, bf16[640,512]{1,0:T(8,128)(2,1)}, f32[320...) custom-call(bf16[320,512]{1,0:T(8,128)(2,1)} %get-tuple-element.50.own_sum, ...), custom_call_target="tpu_custom_call" | custom-call | tf_op jit(solution)/shard_map/pallas_call | solution.py:975
  64.0 77.3 %shard_map.240 = (bf16[2048,512]{1,0:T(8,128)(2,1)}, bf16[2816,512]{1,0:T(8,128)(2,1)}, bf16[1536,512]{1,0:T(8,128)(2,1)}, bf16[640,512]{1,0:T(8,128)(2,1)}, bf16[320,512]{1,0:T(8,128)(2,1)}) custom-call(s32[1]{0:T(128)S(6)} %copy.27.live_ref, bf16[2048,512]{1,0:T(8,128)(2,1)} %lat_ref.3, bf16[2048,512]{1,0:T(8,128)(2,1)} %grad_ref.3, ...), custom_call_target="tpu_custom_call" | custom-call | flops 10737418240 | bytes 14680064 | tf_op jit(solution)/shard_map/pallas_call | solution.py:1013
  141.4 8.3 %shard_map.241 = (bf16[1536,512]{1,0:T(8,128)(2,1)}, bf16[512,512]{1,0:T(8,128)(2,1)}, bf16[640,512]{1,0:T(8,128)(2,1)}, bf16[1024,512]{1,0:T(8,128)(2,1)}, bf16...) custom-call(bf16[2816,512]{1,0:T(8,128)(2,1)} %get-tuple-element.59., ...), custom_call_target="tpu_custom_call" | custom-call | tf_op jit(solution)/shard_map/pallas_call | solution.py:1079

commit v3 on v2

--- a/solution.py
+++ b/solution.py
@@ -215,11 +215,16 @@
     def advance(self, turn):
         count = len(self.order)
         if turn < count:
-            self.reduce_copy(turn).wait()
+            self.reduce_copy(turn).wait_recv()
             self.add(turn)
         else:
-            self.gather_copy(self.gather_order[turn - count]).wait()
+            self.gather_copy(self.gather_order[turn - count]).wait_recv()
         self.begin(turn + 1)
+
+    def drain(self):
+        for stage in range(len(self.order)):
+            self.reduce_copy(stage).wait_send()
+            self.gather_copy(stage).wait_send()
 
 
 def sum_kinds(count):
@@ -360,7 +365,7 @@
         if todo:
             own_piece(todo.pop(0))
         for fold in folds:
-            fold.reduce_copy(stage).wait()
+            fold.reduce_copy(stage).wait_recv()
             fold.add(stage)
             if stage + 1 < count:
                 fold.reduce_copy(stage + 1).start()
@@ -371,7 +376,7 @@
     wide = kinds.count("c")
     for turn in range(wide):
         for fold in folds:
-            fold.gather_copy(fold.gather_order[turn]).wait()
+            fold.gather_copy(fold.gather_order[turn]).wait_recv()
             if turn + 1 < wide:
                 fold.gather_copy(fold.gather_order[turn + 1]).start()
     spans, shares = [], []
@@ -420,10 +425,17 @@
             lo, result = jobs.pop(0)()
             pack[pl.ds(lo, d), :] = (result * factor).astype(BF)
         for number, fold in enumerate(folds):
-            tail_copy(number, fold, turn).wait()
+            tail_copy(number, fold, turn).wait_recv()
             if turn + 1 < count:
                 tail_copy(number, fold, turn + 1).start()
     assert not jobs
+    for number, fold in enumerate(folds):
+        for stage in range(count):
+            fold.reduce_copy(stage).wait_send()
+        for turn in range(wide):
+            fold.gather_copy(fold.gather_order[turn]).wait_send()
+        for turn in tail:
+            tail_copy(number, fold, turn).wait_send()
     node_gain[...] = sum(gains)
 
 
@@ -465,6 +477,7 @@
     proj_s,
     proj_r,
     agg,
+    sums_ref,
     leaving,
     landed,
     send,
@@ -510,24 +523,30 @@
         project(halo_ref[...], own)
 
     send_col, recv_col, _, recv_row = edge_index(tiles_ref, own, halo)
-    rows_in = lat_ref[...]
-    pre = (
-        product(rows_in, win_ref[0])
-        + product(one_hot(send_col, (block, rows), 1), proj_s[...])
-        + product(one_hot(recv_col, (block, rows), 1), proj_r[...])
-    )
-    sig = 1.0 / (1.0 + jnp.exp(-pre))
-    hidden = (pre * sig).astype(BF)
-    slope_ref[...] = (sig * (1.0 + pre * (1.0 - sig))).astype(BF)
-    hid_ref[...] = hidden
-    normed, inverse = normalize(product(hidden, wout_ref[...]))
-    norm_ref[...] = normed.astype(BF)
-    inv_ref[...] = inverse
-    place = step * block + lax.broadcasted_iota(jnp.int32, (block, 1), 0)
-    alive = jnp.where(place < live_ref[0] * tile_width, 1.0, 0.0)
-    message = normed * gain_ref[...] * alive
-    new_ref[...] = (rows_in.astype(F32) + message).astype(BF)
-    agg[...] += product(one_hot(recv_row, (rows, block), 0), message.astype(BF))
+    halves = 2 if block % 256 == 0 else 1
+    half = block // halves
+    for part in range(halves):
+        span = pl.ds(part * half, half)
+        at = slice(part * half, (part + 1) * half)
+        rows_in = lat_ref[span, :]
+        pre = (
+            product(rows_in, win_ref[0])
+            + product(one_hot(send_col[at], (half, rows), 1), proj_s[...])
+            + product(one_hot(recv_col[at], (half, rows), 1), proj_r[...])
+        )
+        sig = 1.0 / (1.0 + jnp.exp(-pre))
+        hidden = (pre * sig).astype(BF)
+        slope_ref[span, :] = (sig * (1.0 + pre * (1.0 - sig))).astype(BF)
+        hid_ref[span, :] = hidden
+        normed, inverse = normalize(product(hidden, wout_ref[...]))
+        norm_ref[span, :] = normed.astype(BF)
+        inv_ref[span, :] = inverse
+        place = step * block + part * half + lax.broadcasted_iota(jnp.int32, (half, 1), 0)
+        alive = jnp.where(place < live_ref[0] * tile_width, 1.0, 0.0)
+        message = normed * gain_ref[...] * alive
+        new_ref[span, :] = (rows_in.astype(F32) + message).astype(BF)
+        sums_ref[span, :] = message.astype(BF)
+    agg[...] += product(one_hot(recv_row, (rows, block), 0), sums_ref[...])
 
     @pl.when(step == pl.num_programs(0) - 1)
     def _():
@@ -646,8 +665,8 @@
                     if wide + turns["n"] < count:
                         share_copy(number, wide + turns["n"]).start()
 
-    table = {0: "n", 2: "n", 3: "n", 5: "na", 7: "na", 8: "b", 9: "a", 10: "nb", 11: "a", 12: "nabcd", 13: "nabcd",
-             14: "nabcd", 15: "nabcd"}
+    table = {0: "n", 3: "n", 6: "n", 7: "a", 9: "n", 10: "b", 11: "a", 12: "cdnab", 13: "cdnab",
+             14: "cdnab", 15: "cdnab"}
 
     @pl.when(step == 0)
     def _():
@@ -780,7 +799,7 @@
             move("n")
         whole_coarse.start()
         while any(turn < 2 * count for turn in turns.values()):
-            move("nabcd")
+            move("cdnab")
         for k in range(len(moves)):
             home_copy(k).wait()
         home = landed[...].reshape(halo, d)
@@ -788,6 +807,7 @@
         for name in groups:
             for fold in groups[name]:
                 fold.delivery().wait()
+                fold.drain()
         whole_coarse.wait()
 
 
@@ -956,6 +976,7 @@
             pltpu.VMEM((rows, d), BF),
             pltpu.VMEM((rows, d), BF),
             pltpu.VMEM((rows, d), F32),
+            pltpu.VMEM((block, d), BF),
         ]
         + swap,
         cost_estimate=cost(2 * edges * d * (3 * rows + 2 * d), 12 * edges * d),
@@ -995,7 +1016,7 @@
     if sum_rows > coarse:
         c_slope = c_slope[:coarse]
     sections = [d, d, coarse + 2, d, d]
-    edge_cuts = [split_rows(section, count, 2) for section in sections]
+    edge_cuts = [split_rows(section, count, pieces) for section, pieces in zip(sections, (2, 2, 3, 4, 2))]
     node_cuts = split_rows(node_rows, count, 3)
     starts = [sum(sum(cuts) for cuts in edge_cuts[:i]) for i in range(len(sections))]
     edge_rows = sum(sum(cuts) for cuts in edge_cuts)

time: 150 us -> 144 us (0.960)
  Pallas kernels: 148 us -> 142 us
    pallas_call x1, Pallas kernels: 77.3 us -> 71.9 us  [on_device(): pl.pallas_call(functools.partial(edge_backward, tile_width, factor, bits,...]
where the time goes in v3:
time: 144 us
  Pallas kernels  142 us (99%)
  between operations  1.47 us (1%)
    pallas_call x1, Pallas kernels, on_device(): pl.pallas_call(functools.partial(edge_backward, tile_width, factor, bits,...  71.9 us
    pallas_call x1, Pallas kernels, on_device(): pl.pallas_call(functools.partial(middle_step, bits, coarse_rows, factor),...  35.3 us
    pallas_call x1, Pallas kernels, on_device(): pl.pallas_call(functools.partial(edge_forward, tile_width, sizes, moves),...  26.7 us
    pallas_call x1, Pallas kernels, on_device(): pl.pallas_call(functools.partial(hand_out, starts, coarse), in_specs=[awa...  8.31 us

profile of v3, /device:TPU:0, one launch (start us, length us, event | category | flops | bytes accessed | tf_op | source)
XLA Modules:
  0.0 143.7 jit_solution(4339532397007427551)
XLA Ops:
  1.3 26.7 %shard_map.238 = (bf16[2048,512]{1,0:T(8,128)(2,1)}, bf16[2048,512]{1,0:T(8,128)(2,1)}, bf16[2048,512]{1,0:T(8,128)(2,1)}, bf16[2048,512]{1,0:T(8,128)(2,1)}, f3...) custom-call(s32[1]{0:T(128)S(6)} %copy.27.live_ref, ...), custom_call_target="tpu_custom_call" | custom-call | flops 8589934592 | bytes 12582912 | tf_op jit(solution)/shard_map/pallas_call | solution.py:963
  28.0 35.3 %shard_map.239 = (bf16[320,512]{1,0:T(8,128)(2,1)}, bf16[80,512]{1,0:T(8,128)(2,1)}, bf16[320,512]{1,0:T(8,128)(2,1)}, bf16[640,512]{1,0:T(8,128)(2,1)}, f32[320...) custom-call(bf16[320,512]{1,0:T(8,128)(2,1)} %get-tuple-element.50.own_sum, ...), custom_call_target="tpu_custom_call" | custom-call | tf_op jit(solution)/shard_map/pallas_call | solution.py:996
  63.3 71.9 %shard_map.240 = (bf16[2048,512]{1,0:T(8,128)(2,1)}, bf16[2816,512]{1,0:T(8,128)(2,1)}, bf16[1536,512]{1,0:T(8,128)(2,1)}, bf16[640,512]{1,0:T(8,128)(2,1)}, bf16[320,512]{1,0:T(8,128)(2,1)}) custom-call(s32[1]{0:T(128)S(6)} %copy.27.live_ref, bf16[2048,512]{1,0:T(8,128)(2,1)} %lat_ref.3, bf16[2048,512]{1,0:T(8,128)(2,1)} %grad_ref.3, ...), custom_call_target="tpu_custom_call" | custom-call | flops 10737418240 | bytes 14680064 | tf_op jit(solution)/shard_map/pallas_call | solution.py:1034
  135.3 8.3 %shard_map.241 = (bf16[1536,512]{1,0:T(8,128)(2,1)}, bf16[512,512]{1,0:T(8,128)(2,1)}, bf16[640,512]{1,0:T(8,128)(2,1)}, bf16[1024,512]{1,0:T(8,128)(2,1)}, bf16...) custom-call(bf16[2816,512]{1,0:T(8,128)(2,1)} %get-tuple-element.59., ...), custom_call_target="tpu_custom_call" | custom-call | tf_op jit(solution)/shard_map/pallas_call | solution.py:1100
